TPU v7x, 256 devices: a whole 4x4x8 slice. The times are simulated.
256 devices in a mesh: seq: 32 (over x, z), head: 8 (over y, core).
Axes of the slice: x: 4, y: 4, z: 8, core: 2. Of those that a mesh axis runs over, the one named last changes fastest.
Arguments:
- inner_input: bfloat16 [16384, 16384], P('seq', 'head'), may hold values from -6 to 6
- state_input: bfloat16 [16384, 4096], P('seq', 'head'), may hold values from -6 to 6
- gate_input: bfloat16 [16384, 16384], P('seq', 'head'), may hold values from -6 to 6
- inner_taps: bfloat16 [4, 16384], P(None, 'head'), may hold values from -3 to 3
- inner_bias: bfloat16 [16384], P('head'), may hold values from -3 to 3
- state_taps: bfloat16 [4, 4096], P(None, 'head'), may hold values from -3 to 3
- state_bias: bfloat16 [4096], P('head'), may hold values from -3 to 3
- step_raw: float32 [256, 16384], P('head', 'seq'), may hold values from -5.3 to -1
- step_bias: float32 [256], P('head'), may hold values from -0.5 to 0.5
- decay_log: float32 [256], P('head'), may hold values from -9 to 1.26
- skip_gain: float32 [256], P('head'), may hold values from 0.5 to 1.5
- norm_gain: bfloat16 [16384], P('head'), may hold values from 0.5 to 1.5
- out_weight: bfloat16 [16384, 4096], P('head', 'seq'), may hold values from -0.09375 to 0.09375
- sequence_lengths: int32 [4], replicated, may hold values from 1 to 8192, 16384 in all
Outputs:
- mixed_out: bfloat16 [16384, 4096], P('seq', 'head')
Inputs may be any that keep to these rules, and one draw needn't show every extreme that they name: `sequence_lengths`: the 4 sequences lie end to end in the order given and fill all 16384 positions; the longest has exactly 8192 positions.
All inputs are finite; a program needn't handle non-finite values.
Results may differ from a plain program's by a relative error of at most 0.018.
Values may be sent and summed in bfloat16 or wider, within the bound.
No kernel may reach another device: no remote copies, remote signals or barrier semaphores. Data moves between devices by JAX's collectives and lax.ppermute only.
A program may use at most 256 MiB of HBM per device.

v0:
```python
from functools import partial

import jax
import jax.numpy as jnp
from jax import lax
from jax.sharding import PartitionSpec as P

HEAD_DIM = 64
STATE_DIM = 256
BLOCK_LEN = 256


HIGHEST = lax.Precision.HIGHEST
EPSILON = 1e-05


def passed_along(value, axis, steps):
    count = lax.axis_size(axis)
    initial, last = (max(0, -steps), min(count, count - steps))
    return lax.ppermute(value, axis, [(source, source + steps) for source in range(initial, last)])


def prefix(array, axis, join, neutral):
    place = lax.axis_index(axis)
    gathered = jax.tree.map(
        lambda a, kind: lax.all_gather(a.astype(kind), axis), array, (jnp.bfloat16, jnp.bfloat16)
    )
    state = jax.tree.map(lambda a, e: jnp.zeros_like(a) + jnp.asarray(e, a.dtype), array, neutral)

    def one(step, state):
        return join(
            state,
            jax.tree.map(
                lambda a, own: lax.dynamic_index_in_dim(a, step, 0, False).astype(own.dtype),
                gathered,
                array,
            ),
        )

    return lax.fori_loop(0, place, one, state)


def segment_of(positions, sequence_lengths):
    starts = jnp.cumsum(sequence_lengths) - sequence_lengths
    hits = (positions[:, None] >= starts[None, :]).astype(jnp.int32)
    return jnp.sum(hits, axis=1) - 1


def causal_conv(extended, seg_extended, tap_table, bias_row):
    tap_count = tap_table.shape[0]
    length = extended.shape[0] - tap_count + 1
    current = seg_extended[tap_count - 1 :]
    summed = jnp.zeros((length, bias_row.shape[0]), jnp.float32) + bias_row.astype(jnp.float32)
    for start_shift in range(tap_count):
        kept_mask = (seg_extended[start_shift : start_shift + length] == current).astype(
            jnp.float32
        )
        summed = (
            summed
            + tap_table[start_shift].astype(jnp.float32)
            * extended[start_shift : start_shift + length].astype(jnp.float32)
            * kept_mask[:, None]
        )
    return jax.nn.silu(summed).astype(jnp.bfloat16)


def block_step(decay_rates, skip_gains, carried, inputs):
    state_now, seg_before = carried
    input_block, write_block, read_block, step_block, seg_block = inputs
    block_rows = input_block.shape[0]
    log_decay = -decay_rates[..., None] * step_block
    running = jnp.cumsum(log_decay, axis=2)
    input_vals = input_block.astype(jnp.float32)
    write_vecs = write_block.astype(jnp.float32)
    read_vecs = read_block.astype(jnp.float32)
    scores = jnp.einsum("ign,jgn->gij", read_vecs, write_vecs, precision=HIGHEST)
    row_index = lax.broadcasted_iota(jnp.int32, (block_rows, block_rows), 0)
    col_index = lax.broadcasted_iota(jnp.int32, (block_rows, block_rows), 1)
    linked = (row_index >= col_index) & (seg_block[:, None] == seg_block[None, :])
    spread = running[..., :, None] - running[..., None, :]
    decays = jnp.where(linked, jnp.exp(jnp.where(linked, spread, 0.0)), 0.0)
    scaled = input_vals * jnp.transpose(step_block, (2, 0, 1))[..., None]
    within = jnp.einsum("ghij,jghp->ighp", decays * scores[:, None], scaled, precision=HIGHEST)
    alive_mask = (seg_block == seg_before).astype(jnp.float32)
    entering = jnp.transpose(alive_mask * jnp.exp(running), (2, 0, 1))
    carried_out = (
        jnp.einsum("ign,ghpn->ighp", read_vecs, state_now, precision=HIGHEST) * entering[..., None]
    )
    outputs = within + carried_out + skip_gains[..., None] * input_vals
    last_seg = seg_block[block_rows - 1]
    closing = (seg_block == last_seg).astype(jnp.float32) * jnp.exp(
        running[..., block_rows - 1 :] - running
    )
    weighted = scaled * jnp.transpose(closing, (2, 0, 1))[..., None]
    kept = (alive_mask[block_rows - 1] * jnp.exp(running[..., block_rows - 1]))[..., None, None]
    new_state = kept * state_now + jnp.einsum(
        "jghp,jgn->ghpn", weighted, write_vecs, precision=HIGHEST
    )
    return ((new_state, last_seg), outputs)


def join_states(earlier, later):
    return (earlier[0] * later[0], later[0][..., None, None] * earlier[1] + later[1])


def per_device(
    inner_input,
    state_input,
    gate_input,
    inner_taps,
    inner_bias,
    state_taps,
    state_bias,
    step_raw,
    step_bias,
    decay_log,
    skip_gain,
    norm_gain,
    out_weight,
    sequence_lengths,
):
    tok_rows = inner_input.shape[0]
    inner_width = inner_input.shape[1]
    head_local = step_raw.shape[0]
    group_local = state_input.shape[1] // (2 * STATE_DIM)
    per_group = head_local // group_local
    tap_count = inner_taps.shape[0]
    block_count = tok_rows // BLOCK_LEN
    first_row = lax.axis_index("seq") * tok_rows
    positions = first_row + lax.iota(jnp.int32, tok_rows + tap_count - 1) - (tap_count - 1)
    seg_extended = segment_of(positions, sequence_lengths)
    seg_local = seg_extended[tap_count - 1 :]
    seg_before = seg_extended[tap_count - 2]
    tail_rows = jnp.concatenate(
        [inner_input[tok_rows - tap_count + 1 :], state_input[tok_rows - tap_count + 1 :]], axis=1
    )
    received = passed_along(tail_rows, "seq", 1)
    inner_conv = causal_conv(
        jnp.concatenate([received[:, :inner_width], inner_input]),
        seg_extended,
        inner_taps,
        inner_bias,
    )
    state_conv = causal_conv(
        jnp.concatenate([received[:, inner_width:], state_input]),
        seg_extended,
        state_taps,
        state_bias,
    )
    inputs_all = inner_conv.reshape(tok_rows, group_local, per_group, HEAD_DIM)
    vectors = state_conv.reshape(tok_rows, group_local, 2, STATE_DIM)
    write_all = vectors[:, :, 0]
    read_all = vectors[:, :, 1]
    steps_all = jax.nn.softplus(step_raw + step_bias[:, None]).reshape(
        group_local, per_group, tok_rows
    )
    decay_rates = jnp.exp(decay_log).reshape(group_local, per_group)
    skip_gains = skip_gain.reshape(group_local, per_group)
    running = jnp.cumsum(-decay_rates[..., None] * steps_all, axis=2)
    alive_mask = (seg_local == seg_before).astype(jnp.float32)
    factor = alive_mask[tok_rows - 1] * jnp.exp(running[..., tok_rows - 1])
    sequence = (
        inputs_all.reshape(block_count, BLOCK_LEN, group_local, per_group, HEAD_DIM),
        write_all.reshape(block_count, BLOCK_LEN, group_local, STATE_DIM),
        read_all.reshape(block_count, BLOCK_LEN, group_local, STATE_DIM),
        jnp.transpose(
            steps_all.reshape(group_local, per_group, block_count, BLOCK_LEN), (2, 0, 1, 3)
        ),
        seg_local.reshape(block_count, BLOCK_LEN),
    )
    stepper = partial(block_step, decay_rates, skip_gains)
    closing = (seg_local == seg_local[tok_rows - 1]).astype(jnp.float32) * jnp.exp(
        running[..., tok_rows - 1 :] - running
    )
    weighted = (
        inputs_all.astype(jnp.float32) * jnp.transpose(steps_all * closing, (2, 0, 1))[..., None]
    )
    local_state = jnp.einsum(
        "tghp,tgn->ghpn", weighted, write_all.astype(jnp.float32), precision=HIGHEST
    )
    factor_in, state_in = prefix(
        (factor, local_state),
        "seq",
        join_states,
        (jnp.ones_like(factor), jnp.zeros_like(local_state)),
    )
    _, outputs = lax.scan(stepper, (state_in, seg_before), sequence)
    y_all = outputs.reshape(tok_rows, group_local, per_group * HEAD_DIM)
    gated = y_all * jax.nn.silu(gate_input.astype(jnp.float32)).reshape(
        tok_rows, group_local, per_group * HEAD_DIM
    )
    mean_sq = jnp.mean(gated * gated, axis=2, keepdims=True)
    gain_rows = norm_gain.astype(jnp.float32).reshape(group_local, per_group * HEAD_DIM)
    normed = (
        (gated * lax.rsqrt(mean_sq + EPSILON) * gain_rows)
        .astype(jnp.bfloat16)
        .reshape(tok_rows, inner_width)
    )
    partial_out = jnp.dot(
        normed,
        lax.all_gather(out_weight, "seq", axis=1, tiled=True),
        preferred_element_type=jnp.float32,
    )
    return lax.psum_scatter(
        partial_out.astype(jnp.bfloat16), "head", scatter_dimension=1, tiled=True
    )


def solution(mesh):
    in_specs = (
        P("seq", "head"),
        P("seq", "head"),
        P("seq", "head"),
        P(None, "head"),
        P("head"),
        P(None, "head"),
        P("head"),
        P("head", "seq"),
        P("head"),
        P("head"),
        P("head"),
        P("head"),
        P("head", "seq"),
        P(),
    )
    out_specs = P("seq", "head")
    return jax.shard_map(
        per_device, mesh=mesh, in_specs=in_specs, out_specs=out_specs, check_vma=False
    )
```

profile of v0, /device:TPU:2, one launch (start us, length us, event | category | flops | bytes accessed | tf_op | source)
XLA Modules:
  0.0 533.5 jit_solution(255418579259593558)
XLA Ops:
  6.5 0.8 slice.134
  7.4 0.7 slice.135
  8.1 3.8 collective-permute-start
  12.6 1.0 broadcast_multiply_fusion.1
  13.6 1.2 reduce-window.34
  15.1 0.8 reduce-window.33
  17.3 1.4 fusion.63
  20.3 0.9 slice_convert_fusion.3
  21.3 0.8 slice_convert_fusion.7
  22.2 2.9 copy.127
  25.4 1.1 copy.126
  26.6 1.4 multiply_convert_fusion.3
  28.0 8.3 %bitcast_multiply_fusion.1 = (f32[512,2048]{0,1:T(8,128)S(1)}, bf16[512,2048]{0,1:T(8,128)(2,1)}) fusion(f32[512,32]{0,1:T(8,128)S(1)} %fusion.62, bf16[512,2048]{0,1:T(8,128)(2,1)S(1)} %copy.127, f32[2048]{0:T(1024)S(1)} %bitcast.259, f32[512]{0:T(512)S(1)} %get-tuple-element.329, bf16[3,2048]{0,1:T(8,128)(2,1)} %copy.126, f32[2048]{0:T(1024)S(1)} %bitcast.260, ...), kind=kLoop, calls=%fused_computation.71 | loop fusion | flops 32505856 | bytes 8513536 | tf_op jit(solution)/shard_map/mul | solution.py:176
  36.3 3.1 convolution_convert_fusion.1
  39.5 0.7 all-gather.5.cloned.1.call-update
  40.4 2.5 copy.141
  42.9 42.2 %all-gather = bf16[32,32,1]{1,2,0:T(2,128)(2,1)S(1)} all-gather(bf16[1,32,1]{1,2,0:T(2,128)(2,1)S(1)} %get-tuple-element.317), channel_id=2, replica_groups=mesh['seq'=32,'head'=8] {'seq'}, dimensions={0}, use_global_device_ids=true | all-gather | bytes 2112 | tf_op jit(solution)/shard_map/all_gather | solution.py:26
  85.1 2.6 reshape_reshape.7
  87.7 1.7 copy.137
  89.7 183.6 %all-gather.7.cloned.1.call-done = bf16[1024,64,256]{2,1,0:T(8,128)(2,1)} async-done(((bf16[32,64,256]{2,1,0:T(8,128)(2,1)}), bf16[1024,64,256]{2,1,0:T(8,128)(2,1)}) %all-gather.7.cloned.1.call-update) | async-done | bytes 33554448 | tf_op jit(solution)/shard_map/all_gather | solution.py:26
  273.6 13.7 %while.28 = (s32[]{:T(128)}, f32[1,32,64,256]{3,2,1,0:T(8,128)S(1)}, s32[]{:T(128)}, bf16[32,1,32]{2,1,0:T(2,128)(2,1)S(1)}, bf16[32,1,32,64,256]{4,3,2,1,0:T(8,128)(2,1)}, /*index=5*/s32[]{:T(128)}, s32[]{:T(128)}, s32[]{:T(128)}) while((s32[]{:T(128)}, f32[1,32,64,256]{3,2,1,0:T(8,128)S(1)}, s32[]{:T(128)}, ...), condition=%wide.region_5.6_spmd, body=%wide.region_4.5_spmd.sunk | while | flops 1572901 | bytes 5243327 | solution.py:40
  273.6 1.6 convert_add_fusion.2
  275.3 1.6 convert_add_fusion.2
  277.0 1.6 convert_add_fusion.2
  278.7 1.6 convert_add_fusion.2
  280.3 1.6 convert_add_fusion.2
  282.0 1.6 convert_add_fusion.2
  283.7 1.6 convert_add_fusion.2
  285.4 1.7 convert_add_fusion.2
  287.3 141.3 %while.29 = (s32[]{:T(128)}, f32[1,32,64,256]{3,2,1,0:T(8,128)S(1)}, s32[]{:T(128)}, f32[2,256,1,32,64]{1,0,4,3,2:T(2,128)}, s32[2,256]{1,0:T(2,128)S(1)}, /*ind...) while((s32[]{:T(128)}, ...), condition=%wide.region_9.10_spmd, body=%wide.region_6.9_spmd.sunk | while | flops 4881359872 | bytes 26427220 | solution.py:187
  288.9 11.8 %fusion.96 = f32[32,64,256]{2,1,0:T(8,128)} fusion(f32[256,256]{1,0:T(8,128)S(1)} %fusion.94, f32[32,256]{1,0:T(8,128)S(1)} %bitcast_add_fusion.6, pred[256,256]{1,0:T(8,128)(4,1)S(1)} %fusion.95, f32[256,32]{0,1:T(8,128)S(1)} %bitcast.240, bf16[2,256,1,32,64]{1,4,3,2,0:T(8,128)(2,1)} %get-tuple-element.503, s32[]{:T(128)} %get-tuple-element.481), kind=kOutput, calls=%fused_computation.2.clone.1 | convolution fusion | flops 1620049920 | bytes 3572224 | tf_op jit(solution)/shard_map/while/body/eval_jaxpr/ghij,jghp->ighp/dot_general | solution.py:83
  302.0 0.7 compare_convert_fusion.4
  302.8 3.1 fusion.97
  306.0 3.5 copy.186
  309.5 42.8 %dynamic_update_slice.7 = f32[2,256,1,32,64]{1,0,4,3,2:T(2,128)} dynamic-update-slice(f32[2,256,1,32,64]{1,0,4,3,2:T(2,128)} %get-tuple-element.484, f32[1,256,1,32,64]{1,0,4,3,2:T(1,128)} %copy.186, s32[]{:T(128)} %get-tuple-element.481, s32[]{:T(128)} %constant.77.clone.1..sunk.1, s32[]{:T(128)} %constant.77.clone.1..sunk.1, s32[]{:T(128)} %constant.77.clone.1..sunk.1, s32[]{:T(128)} %constant.77.clone.1..sunk.1) | dynamic-update-slice | bytes 4194308 | tf_op jit(solution)/shard_map/while/body/jit(dynamic_update_index_in_dim)/dynamic_update_slice | solution.py:187
  353.5 0.7 exponential_multiply_fusion.2
  354.2 3.6 bitcast_add_fusion.5
  359.4 11.8 %fusion.96 = f32[32,64,256]{2,1,0:T(8,128)} fusion(f32[256,256]{1,0:T(8,128)S(1)} %fusion.94, f32[32,256]{1,0:T(8,128)S(1)} %bitcast_add_fusion.6, pred[256,256]{1,0:T(8,128)(4,1)S(1)} %fusion.95, f32[256,32]{0,1:T(8,128)S(1)} %bitcast.240, bf16[2,256,1,32,64]{1,4,3,2,0:T(8,128)(2,1)} %get-tuple-element.503, s32[]{:T(128)} %get-tuple-element.481), kind=kOutput, calls=%fused_computation.2.clone.1 | convolution fusion | flops 1620049920 | bytes 3572224 | tf_op jit(solution)/shard_map/while/body/eval_jaxpr/ghij,jghp->ighp/dot_general | solution.py:83
  372.6 0.7 compare_convert_fusion.4
  373.4 3.1 fusion.97
  376.5 3.5 copy.186
  380.0 42.8 %dynamic_update_slice.7 = f32[2,256,1,32,64]{1,0,4,3,2:T(2,128)} dynamic-update-slice(f32[2,256,1,32,64]{1,0,4,3,2:T(2,128)} %get-tuple-element.484, f32[1,256,1,32,64]{1,0,4,3,2:T(1,128)} %copy.186, s32[]{:T(128)} %get-tuple-element.481, s32[]{:T(128)} %constant.77.clone.1..sunk.1, s32[]{:T(128)} %constant.77.clone.1..sunk.1, s32[]{:T(128)} %constant.77.clone.1..sunk.1, s32[]{:T(128)} %constant.77.clone.1..sunk.1) | dynamic-update-slice | bytes 4194308 | tf_op jit(solution)/shard_map/while/body/jit(dynamic_update_index_in_dim)/dynamic_update_slice | solution.py:187
  424.8 3.6 bitcast_add_fusion.5
  428.6 2.8 copy.157
  431.4 1.9 copy-done
  433.3 1.4 multiply_reduce_fusion
  434.8 16.4 %convolution_convert_fusion = bf16[512,4096]{1,0:T(8,128)(2,1)} fusion(bf16[2048,4096]{1,0:T(8,128)(2,1)} %all-gather.5.cloned.1.call-done, f32[2048]{0:T(1024)S(1)} %convert_element_type.219, f32[512]{0:T(512)S(1)} %add_rsqrt_fusion, f32[512,2048]{0,1:T(8,128)} %bitcast.232, bf16[512,2048]{0,1:T(8,128)(2,1)S(1)} %copy-done.1), kind=kOutput, calls=%fused_computation.64 | convolution fusion | flops 8601468928 | bytes 27273216 | tf_op jit(solution)/shard_map/dot_general | solution.py:199
  451.2 75.7 %reduce-scatter.2.cloned.1.call-done = bf16[512,512]{1,0:T(8,128)(2,1)} async-done(((bf16[512,4096]{1,0:T(8,128)(2,1)}), bf16[512,512]{1,0:T(8,128)(2,1)}) %reduce-scatter.2.cloned.1.call-update) | async-done | bytes 524304 | tf_op jit(solution)/shard_map/reduce_scatter | solution.py:204
  (114 shorter events, 12.4 us)
Async XLA Ops:
  6.5 18.5 %copy-start.3 = (bf16[512,512]{1,0:T(8,128)(2,1)S(1)}, bf16[512,512]{1,0:T(8,128)(2,1)}, u32[]{:S(2)}) copy-start(bf16[512,512]{1,0:T(8,128)(2,1)} %param.19) | copy-start | bytes 1572868
  6.5 18.7 %copy-start.5 = (bf16[2048]{0:T(1024)(128)(2,1)S(1)}, bf16[2048]{0:T(1024)(128)(2,1)}, u32[]{:S(2)}) copy-start(bf16[2048]{0:T(1024)(128)(2,1)} %param.22) | copy-start | bytes 12292
  6.5 18.8 %copy-start.7 = (bf16[512]{0:T(512)(128)(2,1)S(1)}, bf16[512]{0:T(512)(128)(2,1)}, u32[]{:S(2)}) copy-start(bf16[512]{0:T(512)(128)(2,1)} %param.24) | copy-start | bytes 3076
  6.5 266.8 %all-gather.7.cloned.1.call-start = ((), (), s32[]{:S(2)}) async-start(), calls=%async_computation.3 | async-start | bytes 34603008 | tf_op jit(solution)/shard_map/all_gather | solution.py:26
  8.1 17.2 %collective-permute-start = (bf16[3,2560]{1,0:T(4,128)(2,1)S(1)}, bf16[3,2560]{1,0:T(4,128)(2,1)S(1)}, u32[]{:S(2)}, u32[]{:S(2)}) collective-permute-start(bf16[3,2560]{1,0:T(4,128)(2,1)S(1)} %pad_maximum_fusion.2), channel_id=1, source_target_pairs={{0,8},{8,16},{16,24},{24,32},{32,40},{40,48},{48,56},{56,64},{64,7... | collective-permute-start | bytes 46088 | tf_op jit(solution)/shard_map/ppermute | solution.py:20
  36.3 4.1 copy-start.2
  39.4 3.5 copy-start.6
  39.5 395.3 %all-gather.5.cloned.1.call-start = ((), (), s32[]{:S(2)}) async-start(), calls=%async_computation.1 | async-start | bytes 17301504 | tf_op jit(solution)/shard_map/all_gather | solution.py:201
  40.2 486.8 %reduce-scatter.2.cloned.1.call-start = ((), (), s32[]{:S(2)}) async-start(), calls=%async_computation.2 | async-start | bytes 4718592 | tf_op jit(solution)/shard_map/reduce_scatter | solution.py:204
  273.6 13.7 %copy-start.4 = (f32[32]{0:T(128)S(1)}, f32[32]{0:T(128)}, u32[]{:S(2)}) copy-start(f32[32]{0:T(128)} %param.28) | copy-start | bytes 388
  428.6 4.7 copy-start.1
  431.4 1.9 copy-start
Sparse Core Ops, SparseCore 0:
  39.6 233.6 all-gather.6
  275.8 146.3 all-gather.4
  451.3 75.5 reduce-scatter.1
where the time goes:
time: 542 us; the launch traced here: 533 us
  waiting for transfers between devices  260 us (48%)
  local copies, waits for them, and re-layouts  117 us (22%)
  matrix products  56.9 us (10%)
  blocking collectives  42.2 us (8%)
  other arithmetic  36.9 us (7%)
  between operations  14.1 us (3%)
    all_gather x1, waiting for transfers between devices, prefix(): lax.all_gather(a.astype(kind), axis)  184 us
    dynamic_update_slice x4, local copies, waits for them, and re-layouts, per_device(): _, outputs = lax.scan(stepper, (state_in, seg_before), sequence)  92.6 us
    reduce_scatter x1, waiting for transfers between devices, per_device(): lax.psum_scatter(partial_out.astype(jnp.bfloat16), 'head', scatter_dimens...  75.7 us
    all_gather x1, blocking collectives, prefix(): lax.all_gather(a.astype(kind), axis)  42.2 us
    dot_general x2, matrix products, block_step(): jnp.einsum('ghij,jghp->ighp', decays * scores[:, None], scaled, precision...  23.6 us
    dot_general x1, matrix products, per_device(): jnp.dot(normed, lax.all_gather(out_weight, 'seq', axis=1, tiled=True), pr...  16.4 us
    add x8, other arithmetic, join_states(): later[0][..., None, None] * earlier[1] + later[1]  13.2 us
  transfers between devices with their start and end apart: 4, of which 2 were waited for; matrix products, arithmetic and copies ran while one was open for 33% of the time, Pallas kernels for 0%

commit v1 on v0

v1 whole, which is shorter than its diff:
```python
import jax
import jax.numpy as jnp
import numpy as np
from jax import lax
from jax.sharding import Mesh
from jax.sharding import PartitionSpec as P

HEAD_DIM = 64
STATE_DIM = 256
BLOCK_LEN = 256


HIGHEST = lax.Precision.HIGHEST
EPSILON = 1e-05
SEQ = ("sx", "sz")


def segment_of(positions, sequence_lengths):
    starts = jnp.cumsum(sequence_lengths) - sequence_lengths
    hits = (positions[:, None] >= starts[None, :]).astype(jnp.int32)
    return jnp.sum(hits, axis=1) - 1


def causal_conv(extended, seg_extended, tap_table, bias_row):
    tap_count = tap_table.shape[0]
    length = extended.shape[0] - tap_count + 1
    current = seg_extended[tap_count - 1 :]
    summed = jnp.zeros((length, bias_row.shape[0]), jnp.float32) + bias_row.astype(jnp.float32)
    for start_shift in range(tap_count):
        kept_mask = (seg_extended[start_shift : start_shift + length] == current).astype(
            jnp.float32
        )
        summed = (
            summed
            + tap_table[start_shift].astype(jnp.float32)
            * extended[start_shift : start_shift + length].astype(jnp.float32)
            * kept_mask[:, None]
        )
    return jax.nn.silu(summed).astype(jnp.bfloat16)


def exclusive_weights(factors, place):
    n = factors.shape[0]
    idx = jnp.arange(n)
    j = idx[:, None]
    t = idx[None, :]
    between = (t > j) & (t < place)
    prods = jnp.prod(jnp.where(between[:, :, None], factors[None, :, :], 1.0), axis=1)
    return jnp.where((idx < place)[:, None], prods, 0.0)


def pack_state(state, factor):
    heads = factor.shape[0]
    flat = state.reshape(-1, state.shape[-1])
    extra = jnp.zeros((8, flat.shape[1]), jnp.float32).at[0, :heads].set(factor)
    return jnp.concatenate([flat, extra], axis=0).astype(jnp.bfloat16)


def unpack_state(gathered, heads):
    rows = gathered.shape[1] - 8
    states = gathered[:, :rows].astype(jnp.float32).reshape(
        gathered.shape[0], heads, rows // heads, gathered.shape[2]
    )
    factors = gathered[:, rows, :heads].astype(jnp.float32)
    return states, factors


def combine(states, factors, place):
    weights = exclusive_weights(factors, place)
    return jnp.sum(weights[:, :, None, None] * states, axis=0)


def per_device(
    inner_input,
    state_input,
    gate_input,
    inner_taps,
    inner_bias,
    state_taps,
    state_bias,
    step_raw,
    step_bias,
    decay_log,
    skip_gain,
    norm_gain,
    out_weight,
    sequence_lengths,
):
    tok_rows = inner_input.shape[0]
    inner_width = inner_input.shape[1]
    heads = step_raw.shape[0]
    groups = state_input.shape[1] // (2 * STATE_DIM)
    per_group = heads // groups
    tap_count = inner_taps.shape[0]
    chunks = tok_rows // BLOCK_LEN
    L = BLOCK_LEN
    nz = lax.axis_size("sz")
    nseq = lax.axis_size("sx") * nz
    place = lax.axis_index("sx") * nz + lax.axis_index("sz")
    first_row = place * tok_rows

    half = out_weight.shape[0] // 2
    weight_a = lax.all_gather(out_weight[:half], SEQ, axis=1, tiled=True)

    positions = first_row + lax.iota(jnp.int32, tok_rows + tap_count - 1) - (tap_count - 1)
    seg_extended = segment_of(positions, sequence_lengths)
    seg_local = seg_extended[tap_count - 1 :]
    seg_before = seg_extended[tap_count - 2]
    tail_rows = jnp.concatenate(
        [inner_input[tok_rows - tap_count + 1 :], state_input[tok_rows - tap_count + 1 :]], axis=1
    )
    received = lax.ppermute(tail_rows, SEQ, [(s, s + 1) for s in range(nseq - 1)])
    inner_conv = causal_conv(
        jnp.concatenate([received[:, :inner_width], inner_input]),
        seg_extended,
        inner_taps,
        inner_bias,
    )
    state_conv = causal_conv(
        jnp.concatenate([received[:, inner_width:], state_input]),
        seg_extended,
        state_taps,
        state_bias,
    )
    u = inner_conv.reshape(chunks, L, groups, per_group, HEAD_DIM)
    vectors = state_conv.reshape(chunks, L, groups, 2, STATE_DIM)
    write_b = vectors[:, :, :, 0]
    read_c = vectors[:, :, :, 1]
    steps = jax.nn.softplus(step_raw + step_bias[:, None]).reshape(
        groups, per_group, chunks, L
    )
    rates = jnp.exp(decay_log).reshape(groups, per_group)
    gains = skip_gain.reshape(groups, per_group)
    running = jnp.cumsum(-rates[..., None, None] * steps, axis=3)
    seg_c = seg_local.reshape(chunks, L)
    seg_prev = jnp.concatenate([seg_before[None], seg_c[:-1, L - 1]])
    alive = (seg_c == seg_prev[:, None]).astype(jnp.float32)
    last = running[..., L - 1 :]

    u32 = u.astype(jnp.float32)
    scaled = u32 * jnp.transpose(steps, (2, 3, 0, 1))[..., None]

    closing = (seg_c == seg_c[:, L - 1 :]).astype(jnp.float32) * jnp.exp(last - running)
    weighted = scaled * jnp.transpose(closing, (2, 3, 0, 1))[..., None]
    chunk_states = jnp.einsum(
        "cjghp,cjgn->cghpn", weighted, write_b.astype(jnp.float32), precision=HIGHEST
    )
    kept = alive[:, L - 1] * jnp.exp(last[..., 0])
    kept = jnp.transpose(kept, (2, 0, 1))
    shard_state = chunk_states[0]
    shard_factor = kept[0]
    for c in range(1, chunks):
        shard_state = kept[c][..., None, None] * shard_state + chunk_states[c]
        shard_factor = shard_factor * kept[c]

    row = lax.all_gather(pack_state(shard_state, shard_factor.reshape(-1)), "sz")
    row_states, row_factors = unpack_state(row, heads)
    zpos = lax.axis_index("sz")
    in_row = combine(row_states, row_factors, zpos)
    row_decay = jnp.prod(jnp.where((jnp.arange(nz) < zpos)[:, None], row_factors, 1.0), axis=0)
    row_total = combine(row_states, row_factors, nz)
    row_total_factor = jnp.prod(row_factors, axis=0)
    rows = lax.all_gather(pack_state(row_total, row_total_factor), "sx")
    rows_states, rows_factors = unpack_state(rows, heads)
    before_rows = combine(rows_states, rows_factors, lax.axis_index("sx"))
    state_in = (row_decay[:, None, None] * before_rows + in_row).reshape(
        groups, per_group, HEAD_DIM, STATE_DIM
    )

    weight_b_src, rows = lax.optimization_barrier((out_weight[half:], rows))
    weight_b = lax.all_gather(weight_b_src, SEQ, axis=1, tiled=True)

    read32 = read_c.astype(jnp.float32)
    scores = jnp.einsum(
        "cign,cjgn->gcij", read_c, write_b, preferred_element_type=jnp.float32
    )
    row_index = lax.broadcasted_iota(jnp.int32, (L, L), 0)
    col_index = lax.broadcasted_iota(jnp.int32, (L, L), 1)
    linked = (row_index >= col_index)[None] & (seg_c[:, :, None] == seg_c[:, None, :])
    spread = running[..., :, None] - running[..., None, :]
    decays = jnp.where(linked, jnp.exp(jnp.where(linked, spread, 0.0)), 0.0)
    within = jnp.einsum(
        "ghcij,cjghp->cighp", decays * scores[:, None], scaled, precision=HIGHEST
    )

    entering = [state_in]
    for c in range(1, chunks):
        entering.append(kept[c - 1][..., None, None] * entering[-1] + chunk_states[c - 1])
    entering = jnp.stack(entering)
    carried = jnp.einsum("cign,cghpn->cighp", read32, entering, precision=HIGHEST)
    enter_scale = jnp.transpose(alive[None, None] * jnp.exp(running), (2, 3, 0, 1))
    outputs = within + carried * enter_scale[..., None] + gains[..., None] * u32

    y_all = outputs.reshape(tok_rows, groups, per_group * HEAD_DIM)
    gated = y_all * jax.nn.silu(gate_input.astype(jnp.float32)).reshape(
        tok_rows, groups, per_group * HEAD_DIM
    )
    mean_sq = jnp.mean(gated * gated, axis=2, keepdims=True)
    gain_rows = norm_gain.astype(jnp.float32).reshape(groups, per_group * HEAD_DIM)
    normed = (
        (gated * lax.rsqrt(mean_sq + EPSILON) * gain_rows)
        .astype(jnp.bfloat16)
        .reshape(tok_rows, inner_width)
    )
    partial_out = jnp.dot(
        normed[:, :half], weight_a, preferred_element_type=jnp.float32
    ) + jnp.dot(normed[:, half:], weight_b, preferred_element_type=jnp.float32)
    return lax.psum_scatter(
        partial_out.astype(jnp.bfloat16), "head", scatter_dimension=1, tiled=True
    )


def split_seq(mesh):
    seq_devices = mesh.devices[:, 0]
    try:
        nx = len({d.coords[0] for d in seq_devices})
    except AttributeError:
        nx = 1
    nseq = seq_devices.shape[0]
    return Mesh(
        mesh.devices.reshape(nx, nseq // nx, mesh.devices.shape[1]), ("sx", "sz", "head")
    )


def solution(mesh):
    inner = split_seq(mesh)
    in_specs = (
        P(SEQ, "head"),
        P(SEQ, "head"),
        P(SEQ, "head"),
        P(None, "head"),
        P("head"),
        P(None, "head"),
        P("head"),
        P("head", SEQ),
        P("head"),
        P("head"),
        P("head"),
        P("head"),
        P("head", SEQ),
        P(),
    )
    out_specs = P(SEQ, "head")
    return jax.shard_map(
        per_device, mesh=inner, in_specs=in_specs, out_specs=out_specs, check_vma=False
    )
```

time: 542 us -> 484 us (0.89); the launches traced: 533 us -> 483 us
  local copies, waits for them, and re-layouts: 117 us -> 43.7 us
  waiting for transfers between devices: 260 us -> 324 us
  blocking collectives: 42.2 us -> 0 us
  other arithmetic: 36.9 us -> 49.1 us
  matrix products: 56.9 us -> 47.8 us
    all_gather x2 -> x4, waiting for transfers between devices: 184 us -> 283 us  [the longest x1 96.3 us: per_device(): lax.all_gather(pack_state(shard_state, shard_factor.reshape(-1)), 'sz')]
    dynamic_update_slice x4 -> x0, local copies, waits for them, and re-layouts: 92.6 us -> none  [per_device(): _, outputs = lax.scan(stepper, (state_in, seg_before), sequence)]
    all_gather x1 -> x0, blocking collectives: 42.2 us -> none  [prefix(): lax.all_gather(a.astype(kind), axis)]
    reduce_scatter x1, waiting for transfers between devices: 75.7 us -> 40.7 us  [per_device(): lax.psum_scatter(partial_out.astype(jnp.bfloat16), 'head', scatter_dimens...]
    reduce_sum x0 -> x2, other arithmetic: none -> 14.4 us  [combine(): return jnp.sum(weights[:, :, None, None] * states, axis=0)]
    add x8 -> x1, other arithmetic: 13.2 us -> 0.27 us  [per_device(): row_decay[:, None, None] * before_rows + in_row]
    convert_element_type x0 -> x4, local copies, waits for them, and re-layouts: none -> 12.1 us  [the longest x2 11.8 us: per_device(): u32 = u.astype(jnp.float32)]
    dot_general x10 -> x6, matrix products: 56.9 us -> 47.8 us  [the longest x1 21.6 us: per_device(): jnp.einsum('ghcij,cjghp->cighp', decays * scores[:, None], scaled, precis...]
  transfers between devices with their start and end apart: 4 -> 6, of which waited for: 2 -> 5; matrix products, arithmetic and copies ran while one was open for 33% -> 16% of each run, Pallas kernels for 0% -> 0%
where the time goes in v1:
time: 484 us; the launch traced here: 483 us
  waiting for transfers between devices  324 us (67%)
  other arithmetic  49.1 us (10%)
  matrix products  47.8 us (10%)
  local copies, waits for them, and re-layouts  43.7 us (9%)
  between operations  13.6 us (3%)
    all_gather x1, waiting for transfers between devices, per_device(): lax.all_gather(pack_state(shard_state, shard_factor.reshape(-1)), 'sz')  96.3 us
    all_gather x1, waiting for transfers between devices, per_device(): weight_b = lax.all_gather(weight_b_src, SEQ, axis=1, tiled=True)  93.3 us
    all_gather x1, waiting for transfers between devices, per_device(): rows = lax.all_gather(pack_state(row_total, row_total_factor), 'sx')  47 us
    all_gather x1, waiting for transfers between devices, per_device(): weight_a = lax.all_gather(out_weight[:half], SEQ, axis=1, tiled=True)  46.9 us
    reduce_scatter x1, waiting for transfers between devices, per_device(): lax.psum_scatter(partial_out.astype(jnp.bfloat16), 'head', scatter_dimens...  40.7 us
    dot_general x1, matrix products, per_device(): jnp.einsum('ghcij,cjghp->cighp', decays * scores[:, None], scaled, precis...  21.6 us
    unnamed x27, local copies, waits for them, and re-layouts  15.3 us
    reduce_sum x2, other arithmetic, combine(): return jnp.sum(weights[:, :, None, None] * states, axis=0)  14.4 us
  transfers between devices with their start and end apart: 6, of which 5 were waited for; matrix products, arithmetic and copies ran while one was open for 16% of the time, Pallas kernels for 0%

profile of v1, /device:TPU:2, one launch (start us, length us, event | category | flops | bytes accessed | tf_op | source)
XLA Modules:
  0.0 482.6 jit_solution(15707997047912908690)
XLA Ops:
  6.5 0.8 slice.174
  7.3 0.7 slice.175
  8.1 3.8 collective-permute-start
  11.9 0.8 reduce-window.19
  15.0 1.0 compare_select_fusion
  16.8 1.2 reduce-window.20
  18.1 1.4 pad_add_fusion
  20.8 0.9 slice_convert_fusion.3
  21.7 0.8 slice_convert_fusion.8
  23.5 2.9 copy.112
  27.6 6.8 %fusion.28 = f32[512,2048]{0,1:T(8,128)} fusion(bf16[512,2048]{0,1:T(8,128)(2,1)S(1)} %copy.112, f32[2048]{0:T(1024)S(1)} %bitcast.130, f32[512]{0:T(512)S(1)} %get-tuple-element.54, bf16[3,2048]{0,1:T(8,128)(2,1)S(1)} %copy.111, f32[2048]{0:T(1024)S(1)} %bitcast.131, f32[512]{0:T(512)S(1)} %get-tuple-element.55, f32[2048]{0:T(1024)S(1)} %bitcast.129, ...), kind=kLoop, calls=%fused_computation.50 | loop fusion | flops 31457280 | bytes 6350848 | tf_op jit(solution)/shard_map/convert_element_type | solution.py:140
  34.4 6.0 %reshape.768 = f32[2,256,32,64]{1,0,3,2:T(2,128)} reshape(f32[512,2048]{0,1:T(8,128)} %fusion.28) | data formatting | bytes 8388608 | tf_op jit(solution)/shard_map/convert_element_type | solution.py:140
  40.4 0.9 multiply_convert_fusion.2
  41.4 0.7 fusion.54
  42.1 9.1 %broadcast_multiply_fusion = (f32[2,256,32,64]{1,0,3,2:T(2,128)S(1)}, f32[2,256,32,64]{1,0,3,2:T(2,128)}) fusion(f32[2,256,32]{1,0,2:T(2,128)S(1)} %copy.125, f32[2,256,32,64]{1,0,3,2:T(2,128)} %reshape.768, f32[2,256,32]{1,0,2:T(2,128)S(1)} %bitcast.126), kind=kLoop, calls=%fused_computation.48 | loop fusion | flops 2097152 | bytes 12713984 | tf_op jit(solution)/shard_map/mul | solution.py:144
  51.2 2.1 fusion.22
  53.3 2.0 copy-done
  55.5 1.1 pad_maximum_fusion.1
  56.9 96.3 %all-gather.5.cloned.1.call-done = bf16[8,2056,256]{2,1,0:T(8,128)(2,1)} async-done(((bf16[1,2056,256]{2,1,0:T(8,128)(2,1)}), bf16[8,2056,256]{2,1,0:T(8,128)(2,1)}) %all-gather.5.cloned.1.call-update) | async-done | bytes 8421392 | tf_op jit(solution)/shard_map/all_gather | solution.py:156
  153.2 0.7 slice_reduce_fusion.2
  154.5 0.7 mul.529
  155.2 11.2 %fusion = (bf16[2048,256]{1,0:T(8,128)(2,1)S(1)}, f32[2048,256]{1,0:T(8,128)S(1)}) fusion(f32[8,2048]{1,0:T(8,128)S(1)} %mul.520, bf16[8,2056,256]{2,1,0:T(8,128)(2,1)} %all-gather.5.cloned.1.call-done, f32[8,2048]{1,0:T(8,128)} %mul.529), kind=kLoop, calls=%fused_computation.2 | loop fusion | flops 19922944 | bytes 11665408 | tf_op jit(solution)/shard_map/reduce_sum | solution.py:70
  166.4 1.1 pad_maximum_fusion.2
  167.6 1.9 fusion.53
  169.5 47.0 %all-gather.7.cloned.1.call-done = bf16[4,2056,256]{2,1,0:T(8,128)(2,1)} async-done(((bf16[1,2056,256]{2,1,0:T(8,128)(2,1)}), bf16[4,2056,256]{2,1,0:T(8,128)(2,1)}) %all-gather.7.cloned.1.call-update) | async-done | bytes 4210704 | tf_op jit(solution)/shard_map/all_gather | solution.py:163
  216.6 0.7 copy.115
  217.3 0.8 broadcast.372
  218.0 1.0 copy.135
  219.1 1.5 reshape.752
  220.8 3.9 copy.132
  224.7 0.7 convert_element_type.194
  225.6 5.9 %reshape.774 = f32[2,256,1,32,64]{1,0,4,3,2:T(2,128)} reshape(f32[512,2048]{0,1:T(8,128)} %fusion.28) | data formatting | bytes 8388608 | tf_op jit(solution)/shard_map/convert_element_type | solution.py:140
  231.8 21.6 %fusion.2 = f32[2,32,64,256]{3,2,1,0:T(8,128)} fusion(f32[2,256,256]{2,1,0:T(8,128)S(1)} %fusion.36, f32[32,2,256]{2,0,1:T(8,128)S(1)} %reduce_window_sum.47, pred[2,256,256]{2,1,0:T(8,128)(4,1)S(1)} %compare_and_fusion, f32[2,256,32,64]{1,0,3,2:T(2,128)} %get-tuple-element.38), kind=kOutput, calls=%fused_computation.4 | convolution fusion | flops 3238002688 | bytes 9109504 | tf_op jit(solution)/shard_map/ghcij,cjghp->cighp/dot_general | solution.py:182
  253.3 0.7 slice_convert_fusion.4
  254.4 3.2 multiply_reduce_fusion
  257.9 1.9 copy-done.1
  260.3 1.8 copy-done.3
  262.0 1.3 copy-done.4
  263.3 3.0 fusion.21
  266.4 3.4 copy.131
  270.2 1.1 copy-done.2
  271.4 1.4 multiply_reduce_fusion.1
  272.8 1.5 multiply_convert_fusion
  274.3 46.9 %all-gather.9.cloned.1.call-done = bf16[1024,4096]{1,0:T(8,128)(2,1)} async-done(((bf16[1024,128]{1,0:T(8,128)(2,1)}), bf16[1024,4096]{1,0:T(8,128)(2,1)}) %all-gather.9.cloned.1.call-update) | async-done | bytes 8388624 | tf_op jit(solution)/shard_map/all_gather | solution.py:103
  321.1 10.1 %fusion.30 = f32[512,4096]{1,0:T(8,128)} fusion(bf16[1024,4096]{1,0:T(8,128)(2,1)} %all-gather.9.cloned.1.call-done, bf16[512,2048]{0,1:T(8,128)(2,1)S(1)} %multiply_convert_fusion), kind=kOutput, calls=%fused_computation.54 | convolution fusion | flops 4294967296 | bytes 17825792 | tf_op jit(solution)/shard_map/dot_general | solution.py:205
  331.3 93.3 %all-gather.11.cloned.1.call-done = bf16[1024,4096]{1,0:T(8,128)(2,1)} async-done(((bf16[1024,128]{1,0:T(8,128)(2,1)}), bf16[1024,4096]{1,0:T(8,128)(2,1)}) %all-gather.11.cloned.1.call-update) | async-done | bytes 8388624 | tf_op jit(solution)/shard_map/all_gather | solution.py:171
  424.6 10.8 %add_convert_fusion = bf16[512,4096]{1,0:T(8,128)(2,1)} fusion(f32[512,4096]{1,0:T(8,128)} %fusion.30, bf16[1024,4096]{1,0:T(8,128)(2,1)} %all-gather.11.cloned.1.call-done, bf16[512,2048]{0,1:T(8,128)(2,1)S(1)} %multiply_convert_fusion), kind=kOutput, calls=%fused_computation.10 | convolution fusion | flops 4299161600 | bytes 22020096 | tf_op jit(solution)/shard_map/dot_general | solution.py:207
  435.4 40.7 %reduce-scatter.2.cloned.1.call-done = bf16[512,512]{1,0:T(8,128)(2,1)} async-done(((bf16[512,4096]{1,0:T(8,128)(2,1)}), bf16[512,512]{1,0:T(8,128)(2,1)}) %reduce-scatter.2.cloned.1.call-update) | async-done | bytes 524304 | tf_op jit(solution)/shard_map/reduce_scatter | solution.py:208
  (96 shorter events, 10.0 us)
Async XLA Ops:
  6.5 20.7 %copy-start.8 = (bf16[2048]{0:T(1024)(128)(2,1)S(1)}, bf16[2048]{0:T(1024)(128)(2,1)}, u32[]{:S(2)}) copy-start(bf16[2048]{0:T(1024)(128)(2,1)} %param.22) | copy-start | bytes 12292
  6.5 20.7 %copy-start.11 = (bf16[512]{0:T(512)(128)(2,1)S(1)}, bf16[512]{0:T(512)(128)(2,1)}, u32[]{:S(2)}) copy-start(bf16[512]{0:T(512)(128)(2,1)} %param.24) | copy-start | bytes 3076
  6.5 146.7 %all-gather.5.cloned.1.call-start = ((), (), s32[]{:S(2)}) async-start(), calls=%async_computation.1 | async-start | bytes 9474048 | tf_op jit(solution)/shard_map/all_gather | solution.py:156
  8.1 19.2 %collective-permute-start = (bf16[3,2560]{1,0:T(4,128)(2,1)S(1)}, bf16[3,2560]{1,0:T(4,128)(2,1)S(1)}, u32[]{:S(2)}, u32[]{:S(2)}) collective-permute-start(bf16[3,2560]{1,0:T(4,128)(2,1)S(1)} %pad_maximum_fusion.4), channel_id=1, source_target_pairs={{0,8},{8,16},{16,24},{24,32},{32,40},{40,48},{48,56},{56,64},{64,7... | collective-permute-start | bytes 46088 | tf_op jit(solution)/shard_map/ppermute | solution.py:112
  34.4 6.0 %copy-start.5 = (bf16[512,512]{1,0:T(8,128)(2,1)S(1)}, bf16[512,512]{1,0:T(8,128)(2,1)}, u32[]{:S(2)}) copy-start(bf16[512,512]{1,0:T(8,128)(2,1)} %param.19) | copy-start | bytes 1572868
  40.4 1.8 copy-start.6
  53.3 2.0 copy-start
  56.7 159.9 %all-gather.7.cloned.1.call-start = ((), (), s32[]{:S(2)}) async-start(), calls=%async_computation.2 | async-start | bytes 5263360 | tf_op jit(solution)/shard_map/all_gather | solution.py:163
  167.5 153.6 %all-gather.9.cloned.1.call-start = ((), (), s32[]{:S(2)}) async-start(), calls=%async_computation.3 | async-start | bytes 8650752 | tf_op jit(solution)/shard_map/all_gather | solution.py:103
  169.4 255.1 %all-gather.11.cloned.1.call-start = ((), (), s32[]{:S(2)}) async-start(), calls=%async_computation.4 | async-start | bytes 8650752 | tf_op jit(solution)/shard_map/all_gather | solution.py:171
  216.5 259.6 %reduce-scatter.2.cloned.1.call-start = ((), (), s32[]{:S(2)}) async-start(), calls=%async_computation.5 | async-start | bytes 4718592 | tf_op jit(solution)/shard_map/reduce_scatter | solution.py:208
  220.7 4.6 copy-start.7
  257.6 2.2 copy-start.1
  257.6 2.2 copy-start.10
  259.9 2.2 copy-start.3
  259.9 3.5 copy-start.4
  259.9 3.5 copy-start.9
  269.8 1.6 copy-start.2
Sparse Core Ops, SparseCore 0:
  56.8 96.4 all-gather.4
  167.6 48.8 all-gather.6
  219.0 102.1 all-gather.8
  323.5 101.0 all-gather.10
  435.5 40.5 reduce-scatter.1

commit v2 on v1

--- a/solution.py
+++ b/solution.py
@@ -99,8 +99,7 @@
     place = lax.axis_index("sx") * nz + lax.axis_index("sz")
     first_row = place * tok_rows
 
-    half = out_weight.shape[0] // 2
-    weight_a = lax.all_gather(out_weight[:half], SEQ, axis=1, tiled=True)
+    weights = lax.all_gather(out_weight, SEQ, axis=1, tiled=True)
 
     positions = first_row + lax.iota(jnp.int32, tok_rows + tap_count - 1) - (tap_count - 1)
     seg_extended = segment_of(positions, sequence_lengths)
@@ -153,7 +152,10 @@
         shard_state = kept[c][..., None, None] * shard_state + chunk_states[c]
         shard_factor = shard_factor * kept[c]
 
-    row = lax.all_gather(pack_state(shard_state, shard_factor.reshape(-1)), "sz")
+    packed, weights = lax.optimization_barrier(
+        (pack_state(shard_state, shard_factor.reshape(-1)), weights)
+    )
+    row = lax.all_gather(packed, "sz")
     row_states, row_factors = unpack_state(row, heads)
     zpos = lax.axis_index("sz")
     in_row = combine(row_states, row_factors, zpos)
@@ -167,9 +169,6 @@
         groups, per_group, HEAD_DIM, STATE_DIM
     )
 
-    weight_b_src, rows = lax.optimization_barrier((out_weight[half:], rows))
-    weight_b = lax.all_gather(weight_b_src, SEQ, axis=1, tiled=True)
-
     read32 = read_c.astype(jnp.float32)
     scores = jnp.einsum(
         "cign,cjgn->gcij", read_c, write_b, preferred_element_type=jnp.float32
@@ -202,9 +201,7 @@
         .astype(jnp.bfloat16)
         .reshape(tok_rows, inner_width)
     )
-    partial_out = jnp.dot(
-        normed[:, :half], weight_a, preferred_element_type=jnp.float32
-    ) + jnp.dot(normed[:, half:], weight_b, preferred_element_type=jnp.float32)
+    partial_out = jnp.dot(normed, weights, preferred_element_type=jnp.float32)
     return lax.psum_scatter(
         partial_out.astype(jnp.bfloat16), "head", scatter_dimension=1, tiled=True
     )

time: 484 us -> 404 us (0.83)
  waiting for transfers between devices: 324 us -> 254 us
  matrix products: 47.8 us -> 42.6 us
    all_gather x3 -> x2, waiting for transfers between devices: 236 us -> 198 us  [the longest x1 104 us: per_device(): weights = lax.all_gather(out_weight, SEQ, axis=1, tiled=True)]
    all_gather x1, waiting for transfers between devices: 47 us -> 13.5 us  [per_device(): rows = lax.all_gather(pack_state(row_total, row_total_factor), 'sx')]
    dot_general x2 -> x1, matrix products: 20.9 us -> 15.8 us  [per_device(): partial_out = jnp.dot(normed, weights, preferred_element_type=jnp.float32)]
    unnamed x27 -> x29, local copies, waits for them, and re-layouts: 15.3 us -> 15.3 us
  transfers between devices with their start and end apart: 6 -> 5, of which waited for: 5 -> 4; matrix products, arithmetic and copies ran while one was open for 16% -> 20% of each run, Pallas kernels for 0% -> 0%
where the time goes in v2:
time: 404 us; the launch traced here: 403 us
  waiting for transfers between devices  254 us (63%)
  other arithmetic  47.9 us (12%)
  matrix products  42.6 us (11%)
  local copies, waits for them, and re-layouts  40.3 us (10%)
  between operations  13.6 us (3%)
  starting transfers between devices  4.13 us (1%)
    all_gather x1, waiting for transfers between devices, per_device(): weights = lax.all_gather(out_weight, SEQ, axis=1, tiled=True)  104 us
    all_gather x1, waiting for transfers between devices, per_device(): row = lax.all_gather(packed, 'sz')  93.9 us
    reduce_scatter x1, waiting for transfers between devices, per_device(): lax.psum_scatter(partial_out.astype(jnp.bfloat16), 'head', scatter_dimens...  41.7 us
    dot_general x1, matrix products, per_device(): jnp.einsum('ghcij,cjghp->cighp', decays * scores[:, None], scaled, precis...  21.5 us
    dot_general x1, matrix products, per_device(): partial_out = jnp.dot(normed, weights, preferred_element_type=jnp.float32)  15.8 us
    unnamed x29, local copies, waits for them, and re-layouts  15.3 us
    reduce_sum x2, other arithmetic, combine(): return jnp.sum(weights[:, :, None, None] * states, axis=0)  14.4 us
    all_gather x1, waiting for transfers between devices, per_device(): rows = lax.all_gather(pack_state(row_total, row_total_factor), 'sx')  13.5 us
  transfers between devices with their start and end apart: 5, of which 4 were waited for; matrix products, arithmetic and copies ran while one was open for 20% of the time, Pallas kernels for 0%

profile of v2, /device:TPU:2, one launch (start us, length us, event | category | flops | bytes accessed | tf_op | source)
XLA Modules:
  0.0 402.9 jit_solution(4032910775150019644)
XLA Ops:
  6.5 0.7 all-gather.5.cloned.1.call-update
  7.3 0.7 slice.163
  8.0 0.8 slice.162
  8.8 3.8 collective-permute-start
  12.6 0.8 reduce-window.19
  13.5 0.7 bitcast_subtract_fusion
  14.9 1.0 compare_select_fusion
  15.9 0.7 exponential_negate_fusion
  16.6 1.2 reduce-window.20
  18.5 1.3 pad_add_fusion
  21.4 0.8 slice_convert_fusion.8
  22.5 0.9 slice_convert_fusion.3
  24.0 2.9 copy.134
  26.9 0.7 reshape.721
  28.1 6.8 %fusion.31 = f32[512,2048]{0,1:T(8,128)} fusion(bf16[512,2048]{0,1:T(8,128)(2,1)S(1)} %copy.134, f32[2048]{0:T(1024)S(1)} %bitcast.130, f32[512]{0:T(512)S(1)} %get-tuple-element.54, bf16[3,2048]{0,1:T(8,128)(2,1)S(1)} %copy.133, f32[2048]{0:T(1024)S(1)} %bitcast.131, f32[512]{0:T(512)S(1)} %get-tuple-element.55, f32[2048]{0:T(1024)S(1)} %bitcast.129, ...), kind=kLoop, calls=%fused_computation.54 | loop fusion | flops 31457280 | bytes 6350848 | tf_op jit(solution)/shard_map/convert_element_type | solution.py:139
  34.9 5.9 %reshape.740 = f32[2,256,32,64]{1,0,3,2:T(2,128)} reshape(f32[512,2048]{0,1:T(8,128)} %fusion.31) | data formatting | bytes 8388608 | tf_op jit(solution)/shard_map/convert_element_type | solution.py:139
  40.9 0.9 multiply_convert_fusion.3
  41.9 0.7 fusion.55
  42.6 9.1 %broadcast_multiply_fusion = (f32[2,256,32,64]{1,0,3,2:T(2,128)S(1)}, f32[2,256,32,64]{1,0,3,2:T(2,128)}) fusion(f32[2,256,32]{1,0,2:T(2,128)S(1)} %copy.147, f32[2,256,32,64]{1,0,3,2:T(2,128)} %reshape.740, f32[2,256,32]{1,0,2:T(2,128)S(1)} %bitcast.126), kind=kLoop, calls=%fused_computation.52 | loop fusion | flops 2097152 | bytes 12713984 | tf_op jit(solution)/shard_map/mul | solution.py:143
  51.7 2.1 fusion.22
  53.8 1.9 copy-done
  55.9 1.1 fusion.32
  57.0 104.4 %all-gather.5.cloned.1.call-done = bf16[2048,4096]{1,0:T(8,128)(2,1)} async-done(((bf16[2048,128]{1,0:T(8,128)(2,1)}), bf16[2048,4096]{1,0:T(8,128)(2,1)}) %all-gather.5.cloned.1.call-update) | async-done | bytes 16777232 | tf_op jit(solution)/shard_map/all_gather | solution.py:102
  161.8 93.9 %all-gather.9.cloned.1.call-done = bf16[16448,256]{1,0:T(8,128)(2,1)} async-done(((bf16[2056,256]{1,0:T(8,128)(2,1)}), bf16[16448,256]{1,0:T(8,128)(2,1)}) %all-gather.9.cloned.1.call-update) | async-done | bytes 8421392 | tf_op jit(solution)/shard_map/all_gather | solution.py:158
  255.7 0.7 slice_reduce_fusion.2
  256.6 0.7 select_reduce_fusion.3
  257.5 0.7 mul.529
  258.3 11.2 %fusion = (bf16[2048,256]{1,0:T(8,128)(2,1)S(1)}, f32[2048,256]{1,0:T(8,128)S(1)}) fusion(f32[8,2048]{1,0:T(8,128)S(1)} %mul.520, bf16[8,2056,256]{2,1,0:T(8,128)(2,1)} %bitcast.122, f32[8,2048]{1,0:T(8,128)} %mul.529), kind=kLoop, calls=%fused_computation.2 | loop fusion | flops 19922944 | bytes 11665408 | tf_op jit(solution)/shard_map/reduce_sum | solution.py:70
  269.4 1.1 pad_maximum_fusion.1
  270.6 0.7 convert_element_type.187
  271.3 0.7 reshape.723
  272.0 0.8 broadcast.372
  272.8 1.0 copy.157
  274.0 4.0 copy.154
  278.2 6.1 %reshape.746 = f32[2,256,1,32,64]{1,0,4,3,2:T(2,128)} reshape(f32[512,2048]{0,1:T(8,128)} %fusion.31) | data formatting | bytes 8388608 | tf_op jit(solution)/shard_map/convert_element_type | solution.py:139
  284.5 21.5 %fusion.2 = f32[2,32,64,256]{3,2,1,0:T(8,128)} fusion(f32[2,256,256]{2,1,0:T(8,128)S(1)} %fusion.37, f32[32,2,256]{2,0,1:T(8,128)S(1)} %reduce_window_sum.47, pred[2,256,256]{2,1,0:T(8,128)(4,1)S(1)} %compare_and_fusion, f32[2,256,32,64]{1,0,3,2:T(2,128)} %get-tuple-element.40), kind=kOutput, calls=%fused_computation.4 | convolution fusion | flops 3238002688 | bytes 9109504 | tf_op jit(solution)/shard_map/ghcij,cjghp->cighp/dot_general | solution.py:181
  306.0 13.5 %all-gather.7.cloned.1.call-done = bf16[4,2056,256]{2,1,0:T(8,128)(2,1)} async-done(((bf16[1,2056,256]{2,1,0:T(8,128)(2,1)}), bf16[4,2056,256]{2,1,0:T(8,128)(2,1)}) %all-gather.7.cloned.1.call-update) | async-done | bytes 4210704 | tf_op jit(solution)/shard_map/all_gather | solution.py:165
  319.5 0.7 slice_convert_fusion.4
  320.6 3.2 multiply_reduce_fusion
  324.1 1.9 copy-done.1
  326.4 1.8 copy-done.2
  328.2 1.3 copy-done.4
  329.4 3.0 fusion.21
  332.5 3.3 copy.153
  336.3 1.1 copy-done.3
  337.4 1.4 multiply_reduce_fusion.1
  338.9 15.8 %convolution_convert_fusion = bf16[512,4096]{1,0:T(8,128)(2,1)} fusion(bf16[2048,4096]{1,0:T(8,128)(2,1)} %all-gather.5.cloned.1.call-done, f32[2048]{0:T(1024)S(1)} %convert_element_type.187, f32[512]{0:T(512)S(1)} %add_rsqrt_fusion, f32[512,2048]{0,1:T(8,128)S(1)} %bitcast.119, bf16[512,2048]{0,1:T(8,128)(2,1)S(1)} %copy-done.3), kind=kOutput, calls=%fused_computation.16 | convolution fusion | flops 8601468928 | bytes 27273216 | tf_op jit(solution)/shard_map/dot_general | solution.py:204
  354.6 41.7 %reduce-scatter.2.cloned.1.call-done = bf16[512,512]{1,0:T(8,128)(2,1)} async-done(((bf16[512,4096]{1,0:T(8,128)(2,1)}), bf16[512,512]{1,0:T(8,128)(2,1)}) %reduce-scatter.2.cloned.1.call-update) | async-done | bytes 524304 | tf_op jit(solution)/shard_map/reduce_scatter | solution.py:205
  (91 shorter events, 7.7 us)
Async XLA Ops:
  6.5 21.1 %copy-start.9 = (bf16[2048]{0:T(1024)(128)(2,1)S(1)}, bf16[2048]{0:T(1024)(128)(2,1)}, u32[]{:S(2)}) copy-start(bf16[2048]{0:T(1024)(128)(2,1)} %param.22) | copy-start | bytes 12292
  6.5 21.2 %copy-start.12 = (bf16[512]{0:T(512)(128)(2,1)S(1)}, bf16[512]{0:T(512)(128)(2,1)}, u32[]{:S(2)}) copy-start(bf16[512]{0:T(512)(128)(2,1)} %param.24) | copy-start | bytes 3076
  6.5 154.9 %all-gather.5.cloned.1.call-start = ((), (), s32[]{:S(2)}) async-start(), calls=%async_computation.1 | async-start | bytes 17301504 | tf_op jit(solution)/shard_map/all_gather | solution.py:102
  7.3 248.5 %all-gather.9.cloned.1.call-start = ((), (), s32[]{:S(2)}) async-start(), calls=%async_computation.4 | async-start | bytes 9474048 | tf_op jit(solution)/shard_map/all_gather | solution.py:158
  8.8 18.9 %collective-permute-start = (bf16[3,2560]{1,0:T(4,128)(2,1)S(1)}, bf16[3,2560]{1,0:T(4,128)(2,1)S(1)}, u32[]{:S(2)}, u32[]{:S(2)}) collective-permute-start(bf16[3,2560]{1,0:T(4,128)(2,1)S(1)} %pad_maximum_fusion.3), channel_id=1, source_target_pairs={{0,8},{8,16},{16,24},{24,32},{32,40},{40,48},{48,56},{56,64},{64,7... | collective-permute-start | bytes 46088 | tf_op jit(solution)/shard_map/ppermute | solution.py:111
  34.9 6.0 %copy-start.5 = (bf16[512,512]{1,0:T(8,128)(2,1)S(1)}, bf16[512,512]{1,0:T(8,128)(2,1)}, u32[]{:S(2)}) copy-start(bf16[512,512]{1,0:T(8,128)(2,1)} %param.19) | copy-start | bytes 1572868
  40.8 1.8 copy-start.6
  53.7 1.9 copy-start
  161.5 158.0 %all-gather.7.cloned.1.call-start = ((), (), s32[]{:S(2)}) async-start(), calls=%async_computation.2 | async-start | bytes 5263360 | tf_op jit(solution)/shard_map/all_gather | solution.py:165
  270.5 125.8 %reduce-scatter.2.cloned.1.call-start = ((), (), s32[]{:S(2)}) async-start(), calls=%async_computation.3 | async-start | bytes 4718592 | tf_op jit(solution)/shard_map/reduce_scatter | solution.py:205
  273.9 4.0 copy-start.7
  306.0 17.8 %copy-start.8 = (f32[32]{0:T(128)S(1)}, f32[32]{0:T(128)}, u32[]{:S(2)}) copy-start(f32[32]{0:T(128)} %get-tuple-element.61) | copy-start | bytes 388
  323.8 2.2 copy-start.1
  323.8 2.2 copy-start.11
  326.0 2.2 copy-start.2
  326.0 3.5 copy-start.4
  326.0 3.5 copy-start.10
  335.8 1.6 copy-start.3
Sparse Core Ops, SparseCore 0:
  9.8 151.6 all-gather.4
  163.3 92.4 all-gather.8
  270.6 48.8 all-gather.6
  354.8 41.5 reduce-scatter.1

commit v3 on v2

--- a/solution.py
+++ b/solution.py
@@ -63,6 +63,13 @@
     )
     factors = gathered[:, rows, :heads].astype(jnp.float32)
     return states, factors
+
+
+def gather_rows(packed, axis):
+    count = lax.axis_size(axis)
+    return lax.all_to_all(
+        jnp.broadcast_to(packed[None], (count,) + packed.shape), axis, 0, 0, tiled=False
+    )
 
 
 def combine(states, factors, place):
@@ -152,17 +159,14 @@
         shard_state = kept[c][..., None, None] * shard_state + chunk_states[c]
         shard_factor = shard_factor * kept[c]
 
-    packed, weights = lax.optimization_barrier(
-        (pack_state(shard_state, shard_factor.reshape(-1)), weights)
-    )
-    row = lax.all_gather(packed, "sz")
+    row = gather_rows(pack_state(shard_state, shard_factor.reshape(-1)), "sz")
     row_states, row_factors = unpack_state(row, heads)
     zpos = lax.axis_index("sz")
     in_row = combine(row_states, row_factors, zpos)
     row_decay = jnp.prod(jnp.where((jnp.arange(nz) < zpos)[:, None], row_factors, 1.0), axis=0)
     row_total = combine(row_states, row_factors, nz)
     row_total_factor = jnp.prod(row_factors, axis=0)
-    rows = lax.all_gather(pack_state(row_total, row_total_factor), "sx")
+    rows = gather_rows(pack_state(row_total, row_total_factor), "sx")
     rows_states, rows_factors = unpack_state(rows, heads)
     before_rows = combine(rows_states, rows_factors, lax.axis_index("sx"))
     state_in = (row_decay[:, None, None] * before_rows + in_row).reshape(

time: 404 us -> 478 us (1.18)
  waiting for transfers between devices: 254 us -> 309 us
  starting transfers between devices: 4.13 us -> 16.7 us
  local copies, waits for them, and re-layouts: 40.3 us -> 48.5 us
    all_to_all x0 -> x2, waiting for transfers between devices: none -> 260 us  [gather_rows(): lax.all_to_all(jnp.broadcast_to(packed[None], (count,) + packed.shape), a...]
    all_gather x2 -> x0, waiting for transfers between devices: 107 us -> none  [the longest x1 93.9 us: per_device(): row = lax.all_gather(packed, 'sz')]
    all_gather x1, waiting for transfers between devices: 104 us -> 0.02 us  [per_device(): weights = lax.all_gather(out_weight, SEQ, axis=1, tiled=True)]
    all_to_all x0 -> x2, starting transfers between devices: none -> 12.9 us  [gather_rows(): lax.all_to_all(jnp.broadcast_to(packed[None], (count,) + packed.shape), a...]
    reduce_scatter x1, waiting for transfers between devices: 41.7 us -> 48 us  [per_device(): lax.psum_scatter(partial_out.astype(jnp.bfloat16), 'head', scatter_dimens...]
    broadcast_in_dim x0 -> x2, local copies, waits for them, and re-layouts: none -> 5.99 us  [gather_rows(): jnp.broadcast_to(packed[None], (count,) + packed.shape)]
  transfers between devices with their start and end apart: 5 -> 5, of which waited for: 4 -> 3; matrix products, arithmetic and copies ran while one was open for 20% -> 23% of each run, Pallas kernels for 0% -> 0%
where the time goes in v3:
time: 478 us; the launch traced here: 477 us
  waiting for transfers between devices  309 us (65%)
  local copies, waits for them, and re-layouts  48.5 us (10%)
  other arithmetic  45.2 us (9%)
  matrix products  43.5 us (9%)
  starting transfers between devices  16.7 us (3%)
  between operations  13.9 us (3%)
    all_to_all x2, waiting for transfers between devices, gather_rows(): lax.all_to_all(jnp.broadcast_to(packed[None], (count,) + packed.shape), a...  260 us
    reduce_scatter x1, waiting for transfers between devices, per_device(): lax.psum_scatter(partial_out.astype(jnp.bfloat16), 'head', scatter_dimens...  48 us
    dot_general x1, matrix products, per_device(): jnp.einsum('ghcij,cjghp->cighp', decays * scores[:, None], scaled, precis...  21.5 us
    dot_general x1, matrix products, per_device(): partial_out = jnp.dot(normed, weights, preferred_element_type=jnp.float32)  16.7 us
    unnamed x29, local copies, waits for them, and re-layouts  16.2 us
    reduce_sum x2, other arithmetic, combine(): return jnp.sum(weights[:, :, None, None] * states, axis=0)  14.4 us
    all_to_all x2, starting transfers between devices, gather_rows(): lax.all_to_all(jnp.broadcast_to(packed[None], (count,) + packed.shape), a...  12.9 us
    convert_element_type x2, local copies, waits for them, and re-layouts, per_device(): u32 = u.astype(jnp.float32)  11.8 us
  transfers between devices with their start and end apart: 5, of which 3 were waited for; matrix products, arithmetic and copies ran while one was open for 23% of the time, Pallas kernels for 0%

profile of v3, /device:TPU:2, one launch (start us, length us, event | category | flops | bytes accessed | tf_op | source)
XLA Modules:
  0.0 476.6 jit_solution(17819024090575178369)
XLA Ops:
  6.5 0.7 all-gather.2.cloned.1.call-update
  7.3 0.8 slice.162
  8.0 0.7 slice.163
  8.8 3.8 collective-permute-start
  12.6 0.8 reduce-window.19
  14.8 1.0 compare_select_fusion
  15.8 0.7 exponential_negate_fusion
  16.6 1.2 reduce-window.20
  18.5 1.3 pad_add_fusion
  21.3 0.8 slice_convert_fusion.8
  22.5 0.9 slice_convert_fusion.3
  23.9 2.9 copy.117
  26.8 0.7 reshape.719
  28.0 6.8 %fusion.32 = f32[512,2048]{0,1:T(8,128)} fusion(bf16[512,2048]{0,1:T(8,128)(2,1)S(1)} %copy.117, f32[2048]{0:T(1024)S(1)} %bitcast.121, f32[512]{0:T(512)S(1)} %get-tuple-element.50, bf16[3,2048]{0,1:T(8,128)(2,1)S(1)} %copy.116, f32[2048]{0:T(1024)S(1)} %bitcast.122, f32[512]{0:T(512)S(1)} %get-tuple-element.51, f32[2048]{0:T(1024)S(1)} %bitcast.120, ...), kind=kLoop, calls=%fused_computation.55 | loop fusion | flops 31457280 | bytes 6350848 | tf_op jit(solution)/shard_map/convert_element_type | solution.py:146
  34.8 5.9 %reshape.737 = f32[2,256,32,64]{1,0,3,2:T(2,128)} reshape(f32[512,2048]{0,1:T(8,128)} %fusion.32) | data formatting | bytes 8388608 | tf_op jit(solution)/shard_map/convert_element_type | solution.py:146
  40.8 0.9 multiply_convert_fusion.3
  41.8 0.7 fusion.57
  42.5 9.0 %broadcast_multiply_fusion = (f32[2,256,32,64]{1,0,3,2:T(2,128)S(1)}, f32[2,256,32,64]{1,0,3,2:T(2,128)}) fusion(f32[2,256,32]{1,0,2:T(2,128)S(1)} %copy.130, f32[2,256,32,64]{1,0,3,2:T(2,128)} %reshape.737, f32[2,256,32]{1,0,2:T(2,128)S(1)} %bitcast.117), kind=kLoop, calls=%fused_computation.53 | loop fusion | flops 2097152 | bytes 12713984 | tf_op jit(solution)/shard_map/mul | solution.py:150
  51.6 2.1 fusion.22
  53.7 2.0 copy-done
  56.0 3.8 broadcast_in_dim.100
  59.7 7.6 %all-to-all-start = ((bf16[8,2056,256]{2,1,0:T(8,128)(2,1)}), bf16[8,2056,256]{2,1,0:T(8,128)(2,1)}, u32[]{:S(2)}, u32[]{:S(2)}) async-start(bf16[8,2056,256]{2,1,0:T(8,128)(2,1)} %broadcast_in_dim.100), calls=%async_computation | async-start | bytes 16842752 | tf_op jit(solution)/shard_map/all_to_all | solution.py:70
  67.4 249.5 %all-to-all-done = bf16[8,2056,256]{2,1,0:T(8,128)(2,1)} async-done(((bf16[8,2056,256]{2,1,0:T(8,128)(2,1)}), bf16[8,2056,256]{2,1,0:T(8,128)(2,1)}, u32[]{:S(2)}, u32[]{:S(2)}) %all-to-all-start) | async-done | bytes 8421408 | tf_op jit(solution)/shard_map/all_to_all | solution.py:70
  316.9 0.7 slice_reduce_fusion.2
  318.1 0.7 mul.529
  318.8 11.2 %fusion = (bf16[2048,256]{1,0:T(8,128)(2,1)S(1)}, f32[2048,256]{1,0:T(8,128)S(1)}) fusion(f32[8,2048]{1,0:T(8,128)S(1)} %mul.520, bf16[8,2056,256]{2,1,0:T(8,128)(2,1)} %all-to-all-done, f32[8,2048]{1,0:T(8,128)} %mul.529), kind=kLoop, calls=%fused_computation.2 | loop fusion | flops 19922944 | bytes 11665408 | tf_op jit(solution)/shard_map/reduce_sum | solution.py:77
  330.1 2.2 broadcast_in_dim.171
  332.3 5.3 %all-to-all-start.1 = ((bf16[4,2056,256]{2,1,0:T(8,128)(2,1)}), bf16[4,2056,256]{2,1,0:T(8,128)(2,1)}, u32[]{:S(2)}, u32[]{:S(2)}) async-start(bf16[4,2056,256]{2,1,0:T(8,128)(2,1)} %broadcast_in_dim.171), calls=%async_computation.1 | async-start | bytes 8421376 | tf_op jit(solution)/shard_map/all_to_all | solution.py:70
  337.6 0.7 copy.120
  338.3 0.8 broadcast.372
  339.0 1.0 copy.140
  340.1 1.5 reshape.721
  341.7 4.0 copy.137
  345.7 0.7 convert_element_type.188
  346.6 5.9 %reshape.743 = f32[2,256,1,32,64]{1,0,4,3,2:T(2,128)} reshape(f32[512,2048]{0,1:T(8,128)} %fusion.32) | data formatting | bytes 8388608 | tf_op jit(solution)/shard_map/convert_element_type | solution.py:146
  352.8 21.5 %fusion.2 = f32[2,32,64,256]{3,2,1,0:T(8,128)} fusion(f32[2,256,256]{2,1,0:T(8,128)S(1)} %fusion.39, f32[32,2,256]{2,0,1:T(8,128)S(1)} %reduce_window_sum.47, pred[2,256,256]{2,1,0:T(8,128)(4,1)S(1)} %compare_and_fusion, f32[2,256,32,64]{1,0,3,2:T(2,128)} %get-tuple-element.36), kind=kOutput, calls=%fused_computation.4 | convolution fusion | flops 3238002688 | bytes 9109504 | tf_op jit(solution)/shard_map/ghcij,cjghp->cighp/dot_general | solution.py:185
  374.3 10.6 %all-to-all-done.1 = bf16[4,2056,256]{2,1,0:T(8,128)(2,1)} async-done(((bf16[4,2056,256]{2,1,0:T(8,128)(2,1)}), bf16[4,2056,256]{2,1,0:T(8,128)(2,1)}, u32[]{:S(2)}, u32[]{:S(2)}) %all-to-all-start.1) | async-done | bytes 4210720 | tf_op jit(solution)/shard_map/all_to_all | solution.py:70
  384.9 0.7 slice_convert_fusion.4
  386.0 3.2 multiply_reduce_fusion
  389.5 1.9 copy-done.1
  391.8 1.8 copy-done.3
  393.6 1.3 copy-done.5
  394.8 3.0 fusion.21
  397.9 3.4 copy.136
  401.7 1.9 copy-done.2
  403.7 1.4 multiply_reduce_fusion.1
  405.1 16.7 %convolution_convert_fusion = bf16[512,4096]{1,0:T(8,128)(2,1)} fusion(bf16[2048,4096]{1,0:T(8,128)(2,1)} %all-gather.2.cloned.1.call-done, f32[2048]{0:T(1024)S(1)} %convert_element_type.188, f32[512]{0:T(512)S(1)} %add_rsqrt_fusion, f32[512,2048]{0,1:T(8,128)} %bitcast.113, bf16[512,2048]{0,1:T(8,128)(2,1)S(1)} %copy-done.4), kind=kOutput, calls=%fused_computation.16 | convolution fusion | flops 8601468928 | bytes 27273216 | tf_op jit(solution)/shard_map/dot_general | solution.py:208
  421.8 48.0 %reduce-scatter.2.cloned.1.call-done = bf16[512,512]{1,0:T(8,128)(2,1)} async-done(((bf16[512,4096]{1,0:T(8,128)(2,1)}), bf16[512,512]{1,0:T(8,128)(2,1)}) %reduce-scatter.2.cloned.1.call-update) | async-done | bytes 524304 | tf_op jit(solution)/shard_map/reduce_scatter | solution.py:209
  (90 shorter events, 8.2 us)
Async XLA Ops:
  6.5 21.1 %copy-start.9 = (bf16[2048]{0:T(1024)(128)(2,1)S(1)}, bf16[2048]{0:T(1024)(128)(2,1)}, u32[]{:S(2)}) copy-start(bf16[2048]{0:T(1024)(128)(2,1)} %param.22) | copy-start | bytes 12292
  6.5 21.1 %copy-start.12 = (bf16[512]{0:T(512)(128)(2,1)S(1)}, bf16[512]{0:T(512)(128)(2,1)}, u32[]{:S(2)}) copy-start(bf16[512]{0:T(512)(128)(2,1)} %param.24) | copy-start | bytes 3076
  6.5 398.6 %all-gather.2.cloned.1.call-start = ((), (), s32[]{:S(2)}) async-start(), calls=%async_computation.3 | async-start | bytes 17301504 | tf_op jit(solution)/shard_map/all_gather | solution.py:109
  8.8 18.9 %collective-permute-start = (bf16[3,2560]{1,0:T(4,128)(2,1)S(1)}, bf16[3,2560]{1,0:T(4,128)(2,1)S(1)}, u32[]{:S(2)}, u32[]{:S(2)}) collective-permute-start(bf16[3,2560]{1,0:T(4,128)(2,1)S(1)} %pad_maximum_fusion.2), channel_id=1, source_target_pairs={{0,8},{8,16},{16,24},{24,32},{32,40},{40,48},{48,56},{56,64},{64,7... | collective-permute-start | bytes 46088 | tf_op jit(solution)/shard_map/ppermute | solution.py:118
  34.8 5.9 %copy-start.6 = (bf16[512,512]{1,0:T(8,128)(2,1)S(1)}, bf16[512,512]{1,0:T(8,128)(2,1)}, u32[]{:S(2)}) copy-start(bf16[512,512]{1,0:T(8,128)(2,1)} %param.19) | copy-start | bytes 1572868
  40.8 1.8 copy-start.7
  53.7 2.0 copy-start
  59.7 257.1 %all-to-all-start = ((bf16[8,2056,256]{2,1,0:T(8,128)(2,1)}), bf16[8,2056,256]{2,1,0:T(8,128)(2,1)}, u32[]{:S(2)}, u32[]{:S(2)}) async-start(bf16[8,2056,256]{2,1,0:T(8,128)(2,1)} %broadcast_in_dim.100), calls=%async_computation | async-start | bytes 16842752 | tf_op jit(solution)/shard_map/all_to_all | solution.py:70
  332.3 52.6 %all-to-all-start.1 = ((bf16[4,2056,256]{2,1,0:T(8,128)(2,1)}), bf16[4,2056,256]{2,1,0:T(8,128)(2,1)}, u32[]{:S(2)}, u32[]{:S(2)}) async-start(bf16[4,2056,256]{2,1,0:T(8,128)(2,1)} %broadcast_in_dim.171), calls=%async_computation.1 | async-start | bytes 8421376 | tf_op jit(solution)/shard_map/all_to_all | solution.py:70
  337.6 132.2 %reduce-scatter.2.cloned.1.call-start = ((), (), s32[]{:S(2)}) async-start(), calls=%async_computation.4 | async-start | bytes 4718592 | tf_op jit(solution)/shard_map/reduce_scatter | solution.py:209
  341.7 4.7 copy-start.8
  389.2 2.2 copy-start.1
  389.2 2.2 copy-start.11
  391.4 2.2 copy-start.3
  391.4 3.5 copy-start.5
  391.4 3.5 copy-start.10
  401.3 2.4 copy-start.4
  401.7 1.9 copy-start.2
Sparse Core Ops, SparseCore 0:
  9.8 322.7 all-gather.1
  421.9 47.7 reduce-scatter.1

commit v4 on v3

--- a/solution.py
+++ b/solution.py
@@ -106,7 +106,7 @@
     place = lax.axis_index("sx") * nz + lax.axis_index("sz")
     first_row = place * tok_rows
 
-    weights = lax.all_gather(out_weight, SEQ, axis=1, tiled=True)
+    weights_z = lax.all_gather(out_weight, "sz", axis=1, tiled=True)
 
     positions = first_row + lax.iota(jnp.int32, tok_rows + tap_count - 1) - (tap_count - 1)
     seg_extended = segment_of(positions, sequence_lengths)
@@ -159,14 +159,21 @@
         shard_state = kept[c][..., None, None] * shard_state + chunk_states[c]
         shard_factor = shard_factor * kept[c]
 
-    row = gather_rows(pack_state(shard_state, shard_factor.reshape(-1)), "sz")
+    packed, weights_z = lax.optimization_barrier(
+        (pack_state(shard_state, shard_factor.reshape(-1)), weights_z)
+    )
+    weights = lax.all_gather(weights_z, "sx", axis=1, tiled=True)
+    row = gather_rows(packed, "sz")
     row_states, row_factors = unpack_state(row, heads)
     zpos = lax.axis_index("sz")
     in_row = combine(row_states, row_factors, zpos)
     row_decay = jnp.prod(jnp.where((jnp.arange(nz) < zpos)[:, None], row_factors, 1.0), axis=0)
     row_total = combine(row_states, row_factors, nz)
     row_total_factor = jnp.prod(row_factors, axis=0)
-    rows = gather_rows(pack_state(row_total, row_total_factor), "sx")
+    row_pack, weights = lax.optimization_barrier(
+        (pack_state(row_total, row_total_factor), weights)
+    )
+    rows = lax.all_gather(row_pack, "sx")
     rows_states, rows_factors = unpack_state(rows, heads)
     before_rows = combine(rows_states, rows_factors, lax.axis_index("sx"))
     state_in = (row_decay[:, None, None] * before_rows + in_row).reshape(

time: 478 us -> 415 us (0.87)
  waiting for transfers between devices: 309 us -> 257 us
  starting transfers between devices: 16.7 us -> 9.1 us
    all_to_all x2 -> x1, waiting for transfers between devices: 260 us -> 183 us  [gather_rows(): lax.all_to_all(jnp.broadcast_to(packed[None], (count,) + packed.shape), a...]
    all_gather x1 -> x3, waiting for transfers between devices: 0.02 us -> 32 us  [the longest x1 21.1 us: per_device(): weights_z = lax.all_gather(out_weight, 'sz', axis=1, tiled=True)]
    all_to_all x2 -> x1, starting transfers between devices: 12.9 us -> 5.15 us  [gather_rows(): lax.all_to_all(jnp.broadcast_to(packed[None], (count,) + packed.shape), a...]
    reduce_scatter x1, waiting for transfers between devices: 48 us -> 41.7 us  [per_device(): lax.psum_scatter(partial_out.astype(jnp.bfloat16), 'head', scatter_dimens...]
  transfers between devices with their start and end apart: 5 -> 6, of which waited for: 3 -> 4; matrix products, arithmetic and copies ran while one was open for 23% -> 23% of each run, Pallas kernels for 0% -> 0%
where the time goes in v4:
time: 415 us; the launch traced here: 414 us
  waiting for transfers between devices  257 us (62%)
  other arithmetic  47.1 us (11%)
  local copies, waits for them, and re-layouts  44.3 us (11%)
  matrix products  42.6 us (10%)
  between operations  13.6 us (3%)
  starting transfers between devices  9.1 us (2%)
    all_to_all x1, waiting for transfers between devices, gather_rows(): lax.all_to_all(jnp.broadcast_to(packed[None], (count,) + packed.shape), a...  183 us
    reduce_scatter x1, waiting for transfers between devices, per_device(): lax.psum_scatter(partial_out.astype(jnp.bfloat16), 'head', scatter_dimens...  41.7 us
    dot_general x1, matrix products, per_device(): jnp.einsum('ghcij,cjghp->cighp', decays * scores[:, None], scaled, precis...  21.5 us
    all_gather x1, waiting for transfers between devices, per_device(): weights_z = lax.all_gather(out_weight, 'sz', axis=1, tiled=True)  21.1 us
    dot_general x1, matrix products, per_device(): partial_out = jnp.dot(normed, weights, preferred_element_type=jnp.float32)  15.8 us
    unnamed x29, local copies, waits for them, and re-layouts  15.4 us
    reduce_sum x2, other arithmetic, combine(): return jnp.sum(weights[:, :, None, None] * states, axis=0)  14.6 us
    convert_element_type x2, local copies, waits for them, and re-layouts, per_device(): u32 = u.astype(jnp.float32)  12.1 us
  transfers between devices with their start and end apart: 6, of which 4 were waited for; matrix products, arithmetic and copies ran while one was open for 23% of the time, Pallas kernels for 0%

profile of v4, /device:TPU:2, one launch (start us, length us, event | category | flops | bytes accessed | tf_op | source)
XLA Modules:
  0.0 413.6 jit_solution(6615790138665669815)
XLA Ops:
  6.5 0.7 slice.163
  7.2 0.8 slice.162
  8.1 3.8 collective-permute-start
  12.0 0.8 reduce-window.19
  12.8 0.7 bitcast_subtract_fusion
  13.6 0.7 slice.187
  14.3 1.0 compare_select_fusion
  15.3 0.7 exponential_negate_fusion
  16.1 1.2 reduce-window.20
  18.0 1.4 pad_add_fusion
  20.9 0.8 slice_convert_fusion.8
  22.1 0.9 slice_convert_fusion.3
  23.5 2.9 copy.117
  26.4 0.7 reshape.690
  27.6 6.8 %fusion.32 = f32[512,2048]{0,1:T(8,128)} fusion(bf16[512,2048]{0,1:T(8,128)(2,1)S(1)} %copy.117, f32[2048]{0:T(1024)S(1)} %bitcast.124, f32[512]{0:T(512)S(1)} %get-tuple-element.58, bf16[3,2048]{0,1:T(8,128)(2,1)S(1)} %copy.116, f32[2048]{0:T(1024)S(1)} %bitcast.125, f32[512]{0:T(512)S(1)} %get-tuple-element.59, f32[2048]{0:T(1024)S(1)} %bitcast.123, ...), kind=kLoop, calls=%fused_computation.55 | loop fusion | flops 31457280 | bytes 6350848 | tf_op jit(solution)/shard_map/convert_element_type | solution.py:146
  34.3 6.0 %reshape.709 = f32[2,256,32,64]{1,0,3,2:T(2,128)} reshape(f32[512,2048]{0,1:T(8,128)} %fusion.32) | data formatting | bytes 8388608 | tf_op jit(solution)/shard_map/convert_element_type | solution.py:146
  40.3 0.9 multiply_convert_fusion.3
  41.3 0.7 fusion.58
  42.1 9.0 %broadcast_multiply_fusion = (f32[2,256,32,64]{1,0,3,2:T(2,128)S(1)}, f32[2,256,32,64]{1,0,3,2:T(2,128)}) fusion(f32[2,256,32]{1,0,2:T(2,128)S(1)} %copy.130, f32[2,256,32,64]{1,0,3,2:T(2,128)} %reshape.709, f32[2,256,32]{1,0,2:T(2,128)S(1)} %bitcast.120), kind=kLoop, calls=%fused_computation.53 | loop fusion | flops 2097152 | bytes 12713984 | tf_op jit(solution)/shard_map/mul | solution.py:150
  51.1 2.1 fusion.22
  53.2 2.0 copy-done
  55.6 21.1 %all-gather.5.cloned.1.call-done = bf16[2048,1024]{1,0:T(8,128)(2,1)} async-done(((bf16[2048,128]{1,0:T(8,128)(2,1)}), bf16[2048,1024]{1,0:T(8,128)(2,1)}) %all-gather.5.cloned.1.call-update) | async-done | bytes 4194320 | tf_op jit(solution)/shard_map/all_gather | solution.py:109
  76.6 3.8 broadcast_in_dim.100
  80.4 5.1 %all-to-all-start = ((bf16[8,2056,256]{2,1,0:T(8,128)(2,1)}), bf16[8,2056,256]{2,1,0:T(8,128)(2,1)}, u32[]{:S(2)}, u32[]{:S(2)}) async-start(bf16[8,2056,256]{2,1,0:T(8,128)(2,1)} %broadcast_in_dim.100), calls=%async_computation | async-start | bytes 16842752 | tf_op jit(solution)/shard_map/all_to_all | solution.py:70
  85.7 183.0 %all-to-all-done = bf16[8,2056,256]{2,1,0:T(8,128)(2,1)} async-done(((bf16[8,2056,256]{2,1,0:T(8,128)(2,1)}), bf16[8,2056,256]{2,1,0:T(8,128)(2,1)}, u32[]{:S(2)}, u32[]{:S(2)}) %all-to-all-start) | async-done | bytes 8421408 | tf_op jit(solution)/shard_map/all_to_all | solution.py:70
  268.7 0.7 fusion.57
  270.4 0.7 mul.520
  271.2 11.4 %fusion.1 = (f32[2048,256]{1,0:T(8,128)S(1)}, bf16[2048,256]{1,0:T(8,128)(2,1)S(1)}) fusion(f32[8,2048]{1,0:T(8,128)S(1)} %mul.529, bf16[8,2056,256]{2,1,0:T(8,128)(2,1)} %all-to-all-done, f32[8,2048]{1,0:T(8,128)} %mul.520), kind=kLoop, calls=%fused_computation.3 | loop fusion | flops 19922944 | bytes 11665408 | tf_op jit(solution)/shard_map/reduce_sum | solution.py:77
  282.6 1.1 fusion.34
  283.8 0.7 convert_element_type.180
  284.5 0.7 reshape.692
  285.2 0.8 broadcast.373
  285.9 1.0 copy.140
  287.1 4.0 copy.137
  291.3 6.1 %reshape.715 = f32[2,256,1,32,64]{1,0,4,3,2:T(2,128)} reshape(f32[512,2048]{0,1:T(8,128)} %fusion.32) | data formatting | bytes 8388608 | tf_op jit(solution)/shard_map/convert_element_type | solution.py:146
  297.8 21.5 %fusion.2 = f32[2,32,64,256]{3,2,1,0:T(8,128)} fusion(f32[2,256,256]{2,1,0:T(8,128)S(1)} %fusion.39, f32[32,2,256]{2,0,1:T(8,128)S(1)} %reduce_window_sum.47, pred[2,256,256]{2,1,0:T(8,128)(4,1)S(1)} %compare_and_fusion, f32[2,256,32,64]{1,0,3,2:T(2,128)} %get-tuple-element.44), kind=kOutput, calls=%fused_computation.4 | convolution fusion | flops 3238002688 | bytes 9109504 | tf_op jit(solution)/shard_map/ghcij,cjghp->cighp/dot_general | solution.py:192
  319.2 11.0 %all-gather.9.cloned.1.call-done = bf16[8224,256]{1,0:T(8,128)(2,1)} async-done(((bf16[2056,256]{1,0:T(8,128)(2,1)}), bf16[8224,256]{1,0:T(8,128)(2,1)}) %all-gather.9.cloned.1.call-update) | async-done | bytes 4210704 | tf_op jit(solution)/shard_map/all_gather | solution.py:176
  330.2 0.7 slice_convert_fusion.4
  331.3 3.2 multiply_reduce_fusion
  334.8 1.9 copy-done.1
  337.1 1.8 copy-done.2
  338.9 1.3 copy-done.4
  340.1 3.0 fusion.21
  343.2 3.3 copy.136
  347.0 1.1 copy-done.3
  348.1 1.4 multiply_reduce_fusion.1
  349.5 15.8 %convolution_convert_fusion = bf16[512,4096]{1,0:T(8,128)(2,1)} fusion(bf16[2048,4096]{1,0:T(8,128)(2,1)} %all-gather.7.cloned.1.call-done, f32[2048]{0:T(1024)S(1)} %convert_element_type.180, f32[512]{0:T(512)S(1)} %add_rsqrt_fusion, f32[512,2048]{0,1:T(8,128)S(1)} %bitcast.114, bf16[512,2048]{0,1:T(8,128)(2,1)S(1)} %copy-done.3), kind=kOutput, calls=%fused_computation.16 | convolution fusion | flops 8601468928 | bytes 27273216 | tf_op jit(solution)/shard_map/dot_general | solution.py:215
  365.4 41.7 %reduce-scatter.2.cloned.1.call-done = bf16[512,512]{1,0:T(8,128)(2,1)} async-done(((bf16[512,4096]{1,0:T(8,128)(2,1)}), bf16[512,512]{1,0:T(8,128)(2,1)}) %reduce-scatter.2.cloned.1.call-update) | async-done | bytes 524304 | tf_op jit(solution)/shard_map/reduce_scatter | solution.py:216
  (93 shorter events, 7.7 us)
Async XLA Ops:
  6.5 70.1 %all-gather.5.cloned.1.call-start = ((), (), s32[]{:S(2)}) async-start(), calls=%async_computation.2 | async-start | bytes 4718592 | tf_op jit(solution)/shard_map/all_gather | solution.py:109
  8.0 19.2 %copy-start.9 = (bf16[2048]{0:T(1024)(128)(2,1)S(1)}, bf16[2048]{0:T(1024)(128)(2,1)}, u32[]{:S(2)}) copy-start(bf16[2048]{0:T(1024)(128)(2,1)} %param.22) | copy-start | bytes 12292
  8.0 19.2 %copy-start.12 = (bf16[512]{0:T(512)(128)(2,1)S(1)}, bf16[512]{0:T(512)(128)(2,1)}, u32[]{:S(2)}) copy-start(bf16[512]{0:T(512)(128)(2,1)} %param.24) | copy-start | bytes 3076
  8.1 19.2 %collective-permute-start = (bf16[3,2560]{1,0:T(4,128)(2,1)S(1)}, bf16[3,2560]{1,0:T(4,128)(2,1)S(1)}, u32[]{:S(2)}, u32[]{:S(2)}) collective-permute-start(bf16[3,2560]{1,0:T(4,128)(2,1)S(1)} %pad_maximum_fusion.2), channel_id=1, source_target_pairs={{0,8},{8,16},{16,24},{24,32},{32,40},{40,48},{48,56},{56,64},{64,7... | collective-permute-start | bytes 46088 | tf_op jit(solution)/shard_map/ppermute | solution.py:118
  11.9 271.8 %all-gather.7.cloned.1.call-start = ((), (), s32[]{:S(2)}) async-start(), calls=%async_computation.3 | async-start | bytes 20971520 | tf_op jit(solution)/shard_map/all_gather | solution.py:165
  34.3 6.0 %copy-start.5 = (bf16[512,512]{1,0:T(8,128)(2,1)S(1)}, bf16[512,512]{1,0:T(8,128)(2,1)}, u32[]{:S(2)}) copy-start(bf16[512,512]{1,0:T(8,128)(2,1)} %param.19) | copy-start | bytes 1572868
  40.3 1.8 copy-start.6
  53.2 2.0 copy-start
  80.4 188.3 %all-to-all-start = ((bf16[8,2056,256]{2,1,0:T(8,128)(2,1)}), bf16[8,2056,256]{2,1,0:T(8,128)(2,1)}, u32[]{:S(2)}, u32[]{:S(2)}) async-start(bf16[8,2056,256]{2,1,0:T(8,128)(2,1)} %broadcast_in_dim.100), calls=%async_computation | async-start | bytes 16842752 | tf_op jit(solution)/shard_map/all_to_all | solution.py:70
  85.6 244.7 %all-gather.9.cloned.1.call-start = ((), (), s32[]{:S(2)}) async-start(), calls=%async_computation.5 | async-start | bytes 5263360 | tf_op jit(solution)/shard_map/all_gather | solution.py:176
  283.7 123.3 %reduce-scatter.2.cloned.1.call-start = ((), (), s32[]{:S(2)}) async-start(), calls=%async_computation.4 | async-start | bytes 4718592 | tf_op jit(solution)/shard_map/reduce_scatter | solution.py:216
  287.1 4.0 copy-start.7
  319.2 15.3 %copy-start.8 = (f32[32]{0:T(128)S(1)}, f32[32]{0:T(128)}, u32[]{:S(2)}) copy-start(f32[32]{0:T(128)} %get-tuple-element.65) | copy-start | bytes 388
  334.5 2.2 copy-start.1
  334.5 2.2 copy-start.11
  336.7 2.2 copy-start.2
  336.7 3.5 copy-start.4
  336.7 3.5 copy-start.10
  346.5 1.6 copy-start.3
Sparse Core Ops, SparseCore 0:
  12.0 64.5 all-gather.4
  78.4 155.2 all-gather.6
  283.8 46.3 all-gather.8
  365.5 41.5 reduce-scatter.1

commit v5 on v2

--- a/solution.py
+++ b/solution.py
@@ -12,7 +12,8 @@
 
 HIGHEST = lax.Precision.HIGHEST
 EPSILON = 1e-05
-SEQ = ("sx", "sz")
+SEQ = ("sx", "sz1", "sz2")
+LEVELS = ("sz2", "sz1", "sx")
 
 
 def segment_of(positions, sequence_lengths):
@@ -94,9 +95,11 @@
     tap_count = inner_taps.shape[0]
     chunks = tok_rows // BLOCK_LEN
     L = BLOCK_LEN
-    nz = lax.axis_size("sz")
-    nseq = lax.axis_size("sx") * nz
-    place = lax.axis_index("sx") * nz + lax.axis_index("sz")
+    nseq = 1
+    place = 0
+    for name in SEQ:
+        nseq = nseq * lax.axis_size(name)
+        place = place * lax.axis_size(name) + lax.axis_index(name)
     first_row = place * tok_rows
 
     weights = lax.all_gather(out_weight, SEQ, axis=1, tiled=True)
@@ -155,19 +158,25 @@
     packed, weights = lax.optimization_barrier(
         (pack_state(shard_state, shard_factor.reshape(-1)), weights)
     )
-    row = lax.all_gather(packed, "sz")
-    row_states, row_factors = unpack_state(row, heads)
-    zpos = lax.axis_index("sz")
-    in_row = combine(row_states, row_factors, zpos)
-    row_decay = jnp.prod(jnp.where((jnp.arange(nz) < zpos)[:, None], row_factors, 1.0), axis=0)
-    row_total = combine(row_states, row_factors, nz)
-    row_total_factor = jnp.prod(row_factors, axis=0)
-    rows = lax.all_gather(pack_state(row_total, row_total_factor), "sx")
-    rows_states, rows_factors = unpack_state(rows, heads)
-    before_rows = combine(rows_states, rows_factors, lax.axis_index("sx"))
-    state_in = (row_decay[:, None, None] * before_rows + in_row).reshape(
-        groups, per_group, HEAD_DIM, STATE_DIM
-    )
+    state_in = jnp.zeros_like(shard_state)
+    scale = jnp.ones_like(shard_factor)
+    for level, name in enumerate(LEVELS):
+        gathered = lax.all_gather(packed, name)
+        member_states, member_factors = unpack_state(gathered, heads)
+        pos = lax.axis_index(name)
+        count = lax.axis_size(name)
+        state_in = state_in + scale[..., None, None] * combine(
+            member_states, member_factors, pos
+        )
+        scale = scale * jnp.prod(
+            jnp.where((jnp.arange(count) < pos)[:, None], member_factors, 1.0), axis=0
+        )
+        if level + 1 < len(LEVELS):
+            packed = pack_state(
+                combine(member_states, member_factors, count),
+                jnp.prod(member_factors, axis=0),
+            )
+    state_in = state_in.reshape(groups, per_group, HEAD_DIM, STATE_DIM)
 
     read32 = read_c.astype(jnp.float32)
     scores = jnp.einsum(
@@ -214,8 +223,11 @@
     except AttributeError:
         nx = 1
     nseq = seq_devices.shape[0]
+    nz = nseq // nx
+    fine = 4 if nz % 4 == 0 else nz
     return Mesh(
-        mesh.devices.reshape(nx, nseq // nx, mesh.devices.shape[1]), ("sx", "sz", "head")
+        mesh.devices.reshape(nx, nz // fine, fine, mesh.devices.shape[1]),
+        ("sx", "sz1", "sz2", "head"),
     )
 
 

time: 404 us -> 459 us (1.14)
  waiting for transfers between devices: 254 us -> 307 us
    all_gather x2 -> x3, waiting for transfers between devices: 107 us -> 160 us  [per_device(): gathered = lax.all_gather(packed, name)]
    unnamed x29 -> x33, local copies, waits for them, and re-layouts: 15.3 us -> 14.8 us
    reduce_sum x2 -> x3, other arithmetic: 14.4 us -> 14.3 us  [combine(): return jnp.sum(weights[:, :, None, None] * states, axis=0)]
  transfers between devices with their start and end apart: 5 -> 6, of which waited for: 4 -> 5; matrix products, arithmetic and copies ran while one was open for 20% -> 17% of each run, Pallas kernels for 0% -> 0%
where the time goes in v5:
time: 459 us; the launch traced here: 458 us
  waiting for transfers between devices  307 us (67%)
  other arithmetic  51 us (11%)
  matrix products  42.6 us (9%)
  local copies, waits for them, and re-layouts  39.5 us (9%)
  between operations  13.6 us (3%)
    all_gather x3, waiting for transfers between devices, per_device(): gathered = lax.all_gather(packed, name)  160 us
    all_gather x1, waiting for transfers between devices, per_device(): weights = lax.all_gather(out_weight, SEQ, axis=1, tiled=True)  104 us
    reduce_scatter x1, waiting for transfers between devices, per_device(): lax.psum_scatter(partial_out.astype(jnp.bfloat16), 'head', scatter_dimens...  41.7 us
    dot_general x1, matrix products, per_device(): jnp.einsum('ghcij,cjghp->cighp', decays * scores[:, None], scaled, precis...  21.5 us
    dot_general x1, matrix products, per_device(): partial_out = jnp.dot(normed, weights, preferred_element_type=jnp.float32)  15.8 us
    unnamed x33, local copies, waits for them, and re-layouts  14.8 us
    reduce_sum x3, other arithmetic, combine(): return jnp.sum(weights[:, :, None, None] * states, axis=0)  14.3 us
    convert_element_type x2, local copies, waits for them, and re-layouts, per_device(): u32 = u.astype(jnp.float32)  12.1 us
  transfers between devices with their start and end apart: 6, of which 5 were waited for; matrix products, arithmetic and copies ran while one was open for 17% of the time, Pallas kernels for 0%

profile of v5, /device:TPU:2, one launch (start us, length us, event | category | flops | bytes accessed | tf_op | source)
XLA Modules:
  0.0 457.9 jit_solution(7908110028515743954)
XLA Ops:
  6.5 0.7 all-gather.6.cloned.1.call-update
  7.3 0.7 slice.185
  8.0 0.8 slice.184
  8.8 3.8 collective-permute-start
  12.7 0.8 reduce-window.19
  14.9 1.0 compare_select_fusion
  16.6 1.2 reduce-window.20
  18.5 1.3 pad_add_fusion
  21.4 0.8 slice_convert_fusion.8
  22.5 0.9 slice_convert_fusion.3
  24.0 2.9 copy.117
  28.1 6.8 %fusion.33 = f32[512,2048]{0,1:T(8,128)} fusion(bf16[512,2048]{0,1:T(8,128)(2,1)S(1)} %copy.117, f32[2048]{0:T(1024)S(1)} %bitcast.136, f32[512]{0:T(512)S(1)} %get-tuple-element.72, bf16[3,2048]{0,1:T(8,128)(2,1)S(1)} %copy.116, f32[2048]{0:T(1024)S(1)} %bitcast.137, f32[512]{0:T(512)S(1)} %get-tuple-element.73, f32[2048]{0:T(1024)S(1)} %bitcast.135, ...), kind=kLoop, calls=%fused_computation.58 | loop fusion | flops 31457280 | bytes 6350848 | tf_op jit(solution)/shard_map/convert_element_type | solution.py:142
  34.9 6.0 %reshape.955 = f32[2,256,32,64]{1,0,3,2:T(2,128)} reshape(f32[512,2048]{0,1:T(8,128)} %fusion.33) | data formatting | bytes 8388608 | tf_op jit(solution)/shard_map/convert_element_type | solution.py:142
  40.9 0.9 multiply_convert_fusion.3
  41.9 0.7 fusion.58
  42.7 9.2 %broadcast_multiply_fusion = (f32[2,256,32,64]{1,0,3,2:T(2,128)S(1)}, f32[2,256,32,64]{1,0,3,2:T(2,128)}) fusion(f32[2,256,32]{1,0,2:T(2,128)S(1)} %copy.130, f32[2,256,32,64]{1,0,3,2:T(2,128)} %reshape.955, f32[2,256,32]{1,0,2:T(2,128)S(1)} %bitcast.132), kind=kLoop, calls=%fused_computation.56 | loop fusion | flops 2097152 | bytes 12713984 | tf_op jit(solution)/shard_map/mul | solution.py:146
  51.8 2.1 fusion.24
  53.9 2.0 copy-done
  56.1 1.1 fusion.34
  57.2 104.2 %all-gather.6.cloned.1.call-done = bf16[2048,4096]{1,0:T(8,128)(2,1)} async-done(((bf16[2048,128]{1,0:T(8,128)(2,1)}), bf16[2048,4096]{1,0:T(8,128)(2,1)}) %all-gather.6.cloned.1.call-update) | async-done | bytes 16777232 | tf_op jit(solution)/shard_map/all_gather | solution.py:105
  161.8 83.8 %all-gather.12.cloned.1.call-done = bf16[8224,256]{1,0:T(8,128)(2,1)} async-done(((bf16[2056,256]{1,0:T(8,128)(2,1)}), bf16[8224,256]{1,0:T(8,128)(2,1)}) %all-gather.12.cloned.1.call-update) | async-done | bytes 4210704 | tf_op jit(solution)/shard_map/all_gather | solution.py:164
  245.5 0.7 slice_convert_fusion.9
  247.3 6.1 %fusion.6 = (f32[2048,256]{1,0:T(8,128)S(1)}, bf16[2048,256]{1,0:T(8,128)(2,1)S(1)}) fusion(f32[4,2048]{1,0:T(4,128)S(1)} %mul.588, bf16[4,2056,256]{2,1,0:T(8,128)(2,1)} %bitcast.130, f32[4,2048]{1,0:T(4,128)S(1)} %mul.593), kind=kLoop, calls=%fused_computation.8 | loop fusion | flops 9437184 | bytes 7405568 | tf_op jit(solution)/shard_map/reduce_sum | solution.py:71
  253.4 1.1 pad_maximum_fusion.1
  254.6 65.6 %all-gather.8.cloned.1.call-done = bf16[2,2056,256]{2,1,0:T(8,128)(2,1)} async-done(((bf16[1,2056,256]{2,1,0:T(8,128)(2,1)}), bf16[2,2056,256]{2,1,0:T(8,128)(2,1)}) %all-gather.8.cloned.1.call-update) | async-done | bytes 2105360 | tf_op jit(solution)/shard_map/all_gather | solution.py:164
  320.2 0.7 slice_convert_fusion.10
  322.0 4.8 %fusion.13 = (f32[2048,256]{1,0:T(8,128)}, bf16[2048,256]{1,0:T(8,128)(2,1)S(1)}) fusion(f32[2,2048]{1,0:T(2,128)S(1)} %mul.597, bf16[2,2056,256]{2,1,0:T(8,128)(2,1)} %all-gather.8.cloned.1.call-done, f32[2,2048]{1,0:T(2,128)S(1)} %mul.604), kind=kLoop, calls=%fused_computation.21 | loop fusion | flops 4194304 | bytes 5275648 | tf_op jit(solution)/shard_map/reduce_sum | solution.py:71
  326.8 1.0 pad_maximum_fusion.2
  328.0 0.7 convert_element_type.211
  328.7 0.7 reshape.937
  329.4 0.8 broadcast.487
  330.2 1.0 copy.139
  331.3 4.0 copy.136
  335.6 6.2 %reshape.961 = f32[2,256,1,32,64]{1,0,4,3,2:T(2,128)} reshape(f32[512,2048]{0,1:T(8,128)} %fusion.33) | data formatting | bytes 8388608 | tf_op jit(solution)/shard_map/convert_element_type | solution.py:142
  342.0 21.5 %fusion = f32[2,32,64,256]{3,2,1,0:T(8,128)} fusion(f32[2,256,256]{2,1,0:T(8,128)S(1)} %fusion.39, f32[32,2,256]{2,0,1:T(8,128)S(1)} %reduce_window_sum.47, pred[2,256,256]{2,1,0:T(8,128)(4,1)S(1)} %compare_and_fusion, f32[2,256,32,64]{1,0,3,2:T(2,128)} %get-tuple-element.56), kind=kOutput, calls=%fused_computation | convolution fusion | flops 3238002688 | bytes 9109504 | tf_op jit(solution)/shard_map/ghcij,cjghp->cighp/dot_general | solution.py:190
  363.5 10.9 %all-gather.10.cloned.1.call-done = bf16[4,2056,256]{2,1,0:T(8,128)(2,1)} async-done(((bf16[1,2056,256]{2,1,0:T(8,128)(2,1)}), bf16[4,2056,256]{2,1,0:T(8,128)(2,1)}) %all-gather.10.cloned.1.call-update) | async-done | bytes 4210704 | tf_op jit(solution)/shard_map/all_gather | solution.py:164
  374.4 0.7 slice_convert_fusion.4
  375.5 3.4 multiply_reduce_fusion
  379.4 1.6 copy-done.1
  381.1 0.8 add_bitcast_fusion
  381.8 1.4 copy-done.3
  383.2 1.3 copy-done.5
  384.5 3.0 fusion.23
  387.5 3.3 copy.135
  391.3 1.1 copy-done.4
  392.5 1.4 multiply_reduce_fusion.1
  393.9 15.8 %convolution_convert_fusion = bf16[512,4096]{1,0:T(8,128)(2,1)} fusion(bf16[2048,4096]{1,0:T(8,128)(2,1)} %all-gather.6.cloned.1.call-done, f32[2048]{0:T(1024)S(1)} %convert_element_type.211, f32[512]{0:T(512)S(1)} %add_rsqrt_fusion, f32[512,2048]{0,1:T(8,128)S(1)} %bitcast.124, bf16[512,2048]{0,1:T(8,128)(2,1)S(1)} %copy-done.4), kind=kOutput, calls=%fused_computation.16 | convolution fusion | flops 8601468928 | bytes 27273216 | tf_op jit(solution)/shard_map/dot_general | solution.py:213
  409.7 41.7 %reduce-scatter.2.cloned.1.call-done = bf16[512,512]{1,0:T(8,128)(2,1)} async-done(((bf16[512,4096]{1,0:T(8,128)(2,1)}), bf16[512,512]{1,0:T(8,128)(2,1)}) %reduce-scatter.2.cloned.1.call-update) | async-done | bytes 524304 | tf_op jit(solution)/shard_map/reduce_scatter | solution.py:214
  (112 shorter events, 11.5 us)
Async XLA Ops:
  6.5 21.2 %copy-start.10 = (bf16[2048]{0:T(1024)(128)(2,1)S(1)}, bf16[2048]{0:T(1024)(128)(2,1)}, u32[]{:S(2)}) copy-start(bf16[2048]{0:T(1024)(128)(2,1)} %param.24) | copy-start | bytes 12292
  6.5 21.2 %copy-start.13 = (bf16[512]{0:T(512)(128)(2,1)S(1)}, bf16[512]{0:T(512)(128)(2,1)}, u32[]{:S(2)}) copy-start(bf16[512]{0:T(512)(128)(2,1)} %param.26) | copy-start | bytes 3076
  6.5 154.9 %all-gather.6.cloned.1.call-start = ((), (), s32[]{:S(2)}) async-start(), calls=%async_computation.1 | async-start | bytes 17301504 | tf_op jit(solution)/shard_map/all_gather | solution.py:105
  7.3 238.3 %all-gather.12.cloned.1.call-start = ((), (), s32[]{:S(2)}) async-start(), calls=%async_computation.5 | async-start | bytes 5263360 | tf_op jit(solution)/shard_map/all_gather | solution.py:164
  8.8 19.0 %collective-permute-start = (bf16[3,2560]{1,0:T(4,128)(2,1)S(1)}, bf16[3,2560]{1,0:T(4,128)(2,1)S(1)}, u32[]{:S(2)}, u32[]{:S(2)}) collective-permute-start(bf16[3,2560]{1,0:T(4,128)(2,1)S(1)} %pad_maximum_fusion.4), channel_id=1, source_target_pairs={{0,8},{8,16},{16,24},{24,32},{32,40},{40,48},{48,56},{56,64},{64,7... | collective-permute-start | bytes 46088 | tf_op jit(solution)/shard_map/ppermute | solution.py:114
  34.9 6.0 %copy-start.6 = (bf16[512,512]{1,0:T(8,128)(2,1)S(1)}, bf16[512,512]{1,0:T(8,128)(2,1)}, u32[]{:S(2)}) copy-start(bf16[512,512]{1,0:T(8,128)(2,1)} %param.21) | copy-start | bytes 1572868
  40.9 1.8 copy-start.7
  53.9 2.0 copy-start
  161.5 158.7 %all-gather.8.cloned.1.call-start = ((), (), s32[]{:S(2)}) async-start(), calls=%async_computation.2 | async-start | bytes 3158016 | tf_op jit(solution)/shard_map/all_gather | solution.py:164
  254.5 119.9 %all-gather.10.cloned.1.call-start = ((), (), s32[]{:S(2)}) async-start(), calls=%async_computation.3 | async-start | bytes 5263360 | tf_op jit(solution)/shard_map/all_gather | solution.py:164
  327.9 123.5 %reduce-scatter.2.cloned.1.call-start = ((), (), s32[]{:S(2)}) async-start(), calls=%async_computation.4 | async-start | bytes 4718592 | tf_op jit(solution)/shard_map/reduce_scatter | solution.py:214
  331.3 4.0 copy-start.8
  342.0 21.5 %copy-start.9 = (f32[32]{0:T(128)S(1)}, f32[32]{0:T(128)}, u32[]{:S(2)}) copy-start(f32[32]{0:T(128)} %get-tuple-element.81) | copy-start | bytes 388
  342.0 21.5 %copy-start.14 = (f32[32]{0:T(128)S(1)}, f32[32]{0:T(128)}, u32[]{:S(2)}) copy-start(f32[32]{0:T(128)} %get-tuple-element.79) | copy-start | bytes 388
  375.5 3.4 copy-start.2
  378.9 2.2 copy-start.1
  378.9 2.2 copy-start.12
  381.0 2.2 copy-start.3
  381.0 3.5 copy-start.5
  381.1 3.5 copy-start.11
  390.9 1.6 copy-start.4
Sparse Core Ops, SparseCore 0:
  9.8 151.6 all-gather.5
  163.3 82.2 all-gather.11
  254.6 65.4 all-gather.7
  328.0 46.3 all-gather.9
  409.8 41.5 reduce-scatter.1

commit v6 on v2

--- a/solution.py
+++ b/solution.py
@@ -158,11 +158,15 @@
     row = lax.all_gather(packed, "sz")
     row_states, row_factors = unpack_state(row, heads)
     zpos = lax.axis_index("sz")
+    row_total = combine(row_states, row_factors, nz)
+    row_total_factor = jnp.prod(row_factors, axis=0)
+    row_pack = pack_state(row_total, row_total_factor)
+    row_states, row_factors, row_pack = lax.optimization_barrier(
+        (row_states, row_factors, row_pack)
+    )
+    rows = lax.all_gather(row_pack, "sx")
     in_row = combine(row_states, row_factors, zpos)
     row_decay = jnp.prod(jnp.where((jnp.arange(nz) < zpos)[:, None], row_factors, 1.0), axis=0)
-    row_total = combine(row_states, row_factors, nz)
-    row_total_factor = jnp.prod(row_factors, axis=0)
-    rows = lax.all_gather(pack_state(row_total, row_total_factor), "sx")
     rows_states, rows_factors = unpack_state(rows, heads)
     before_rows = combine(rows_states, rows_factors, lax.axis_index("sx"))
     state_in = (row_decay[:, None, None] * before_rows + in_row).reshape(

time: 404 us -> 407 us (level)
  other arithmetic: 47.9 us -> 59.6 us
  waiting for transfers between devices: 254 us -> 248 us
    convert_element_type x0 -> x1, other arithmetic: none -> 10.6 us  [unpack_state(): gathered[:, :rows].astype(jnp.float32)]
    all_gather x1, waiting for transfers between devices: 13.5 us -> 7.59 us  [per_device(): rows = lax.all_gather(row_pack, 'sx')]
    reduce_sum x2 -> x3, other arithmetic: 14.4 us -> 15.9 us  [combine(): return jnp.sum(weights[:, :, None, None] * states, axis=0)]
    unnamed x29 -> x35, local copies, waits for them, and re-layouts: 15.3 us -> 13.9 us
  transfers between devices with their start and end apart: 5 -> 5, of which waited for: 4 -> 4; matrix products, arithmetic and copies ran while one was open for 20% -> 21% of each run, Pallas kernels for 0% -> 0%
where the time goes in v6:
time: 407 us; the launch traced here: 406 us
  waiting for transfers between devices  248 us (61%)
  other arithmetic  59.6 us (15%)
  matrix products  42.7 us (10%)
  local copies, waits for them, and re-layouts  37.9 us (9%)
  between operations  13.6 us (3%)
  starting transfers between devices  4.13 us (1%)
    all_gather x1, waiting for transfers between devices, per_device(): weights = lax.all_gather(out_weight, SEQ, axis=1, tiled=True)  104 us
    all_gather x1, waiting for transfers between devices, per_device(): row = lax.all_gather(packed, 'sz')  94 us
    reduce_scatter x1, waiting for transfers between devices, per_device(): lax.psum_scatter(partial_out.astype(jnp.bfloat16), 'head', scatter_dimens...  41.6 us
    dot_general x1, matrix products, per_device(): jnp.einsum('ghcij,cjghp->cighp', decays * scores[:, None], scaled, precis...  21.6 us
    reduce_sum x3, other arithmetic, combine(): return jnp.sum(weights[:, :, None, None] * states, axis=0)  15.9 us
    dot_general x1, matrix products, per_device(): partial_out = jnp.dot(normed, weights, preferred_element_type=jnp.float32)  15.8 us
    unnamed x35, local copies, waits for them, and re-layouts  13.9 us
    convert_element_type x2, local copies, waits for them, and re-layouts, per_device(): u32 = u.astype(jnp.float32)  11.9 us
  transfers between devices with their start and end apart: 5, of which 4 were waited for; matrix products, arithmetic and copies ran while one was open for 21% of the time, Pallas kernels for 0%

profile of v6, /device:TPU:2, one launch (start us, length us, event | category | flops | bytes accessed | tf_op | source)
XLA Modules:
  0.0 406.3 jit_solution(4577869035277629661)
XLA Ops:
  6.5 0.7 all-gather.6.cloned.1.call-update
  7.3 0.7 slice.163
  8.0 0.8 slice.162
  8.8 3.8 collective-permute-start
  12.6 0.8 reduce-window.19
  13.5 0.7 bitcast_subtract_fusion
  14.9 1.0 compare_select_fusion
  15.9 0.7 exponential_negate_fusion
  16.6 1.2 reduce-window.20
  18.5 1.3 pad_add_fusion
  21.4 0.8 slice_convert_fusion.9
  22.5 0.9 slice_convert_fusion.4
  23.4 0.6 slice_bitcast_fusion.2
  24.0 2.9 copy.133
  27.0 0.7 reshape.682
  28.1 6.8 %fusion.33 = f32[512,2048]{0,1:T(8,128)} fusion(bf16[512,2048]{0,1:T(8,128)(2,1)S(1)} %copy.133, f32[2048]{0:T(1024)S(1)} %bitcast.134, f32[512]{0:T(512)S(1)} %get-tuple-element.56, bf16[3,2048]{0,1:T(8,128)(2,1)S(1)} %copy.132, f32[2048]{0:T(1024)S(1)} %bitcast.135, f32[512]{0:T(512)S(1)} %get-tuple-element.57, f32[2048]{0:T(1024)S(1)} %bitcast.133, ...), kind=kLoop, calls=%fused_computation.57 | loop fusion | flops 31457280 | bytes 6350848 | tf_op jit(solution)/shard_map/convert_element_type | solution.py:139
  34.9 6.0 %reshape.702 = f32[2,256,32,64]{1,0,3,2:T(2,128)} reshape(f32[512,2048]{0,1:T(8,128)} %fusion.33) | data formatting | bytes 8388608 | tf_op jit(solution)/shard_map/convert_element_type | solution.py:139
  40.9 0.9 multiply_convert_fusion.3
  41.9 0.7 fusion.58
  42.6 9.1 %broadcast_multiply_fusion = (f32[2,256,32,64]{1,0,3,2:T(2,128)S(1)}, f32[2,256,32,64]{1,0,3,2:T(2,128)}) fusion(f32[2,256,32]{1,0,2:T(2,128)S(1)} %copy.146, f32[2,256,32,64]{1,0,3,2:T(2,128)} %reshape.702, f32[2,256,32]{1,0,2:T(2,128)S(1)} %bitcast.130), kind=kLoop, calls=%fused_computation.55 | loop fusion | flops 2097152 | bytes 12713984 | tf_op jit(solution)/shard_map/mul | solution.py:143
  51.8 2.1 fusion.20
  53.8 1.9 copy-done
  56.0 1.1 fusion.34
  57.1 104.4 %all-gather.6.cloned.1.call-done = bf16[2048,4096]{1,0:T(8,128)(2,1)} async-done(((bf16[2048,128]{1,0:T(8,128)(2,1)}), bf16[2048,4096]{1,0:T(8,128)(2,1)}) %all-gather.6.cloned.1.call-update) | async-done | bytes 16777232 | tf_op jit(solution)/shard_map/all_gather | solution.py:102
  161.7 94.0 %all-gather.8.cloned.1.call-done = bf16[16448,256]{1,0:T(8,128)(2,1)} async-done(((bf16[2056,256]{1,0:T(8,128)(2,1)}), bf16[16448,256]{1,0:T(8,128)(2,1)}) %all-gather.8.cloned.1.call-update) | async-done | bytes 8421392 | tf_op jit(solution)/shard_map/all_gather | solution.py:158
  255.7 10.6 %slice_convert_fusion = f32[8,2048,256]{2,1,0:T(8,128)} fusion(bf16[8,2056,256]{2,1,0:T(8,128)(2,1)} %bitcast.118), kind=kLoop, calls=%fused_computation.8 | loop fusion | flops 4194304 | bytes 25165824 | tf_op jit(solution)/shard_map/convert_element_type | solution.py:61
  266.3 0.7 slice_reduce_fusion.2
  267.5 5.5 %multiply_reduce_fusion.1 = bf16[2048,256]{1,0:T(8,128)(2,1)S(1)} fusion(f32[8,2048]{1,0:T(8,128)S(1)} %mul.514, bf16[8,2056,256]{2,1,0:T(8,128)(2,1)} %bitcast.120), kind=kLoop, calls=%fused_computation.1 | loop fusion | flops 12058624 | bytes 9502720 | tf_op jit(solution)/shard_map/reduce_sum | solution.py:70
  272.9 1.1 fusion.35
  274.7 0.7 reshape.684
  275.4 0.8 broadcast.371
  276.2 1.0 copy.156
  277.4 2.5 copy.153
  280.2 6.0 %reshape.708 = f32[2,256,1,32,64]{1,0,4,3,2:T(2,128)} reshape(f32[512,2048]{0,1:T(8,128)} %fusion.33) | data formatting | bytes 8388608 | tf_op jit(solution)/shard_map/convert_element_type | solution.py:139
  286.4 21.6 %fusion = f32[2,32,64,256]{3,2,1,0:T(8,128)} fusion(f32[2,256,256]{2,1,0:T(8,128)S(1)} %fusion.40, f32[32,2,256]{2,0,1:T(8,128)S(1)} %reduce_window_sum.47, pred[2,256,256]{2,1,0:T(8,128)(4,1)S(1)} %compare_and_fusion, f32[2,256,32,64]{1,0,3,2:T(2,128)} %get-tuple-element.42), kind=kOutput, calls=%fused_computation.2 | convolution fusion | flops 3238002688 | bytes 9109504 | tf_op jit(solution)/shard_map/ghcij,cjghp->cighp/dot_general | solution.py:185
  308.2 7.3 %multiply_reduce_fusion = f32[32,64,256]{2,1,0:T(8,128)S(1)} fusion(f32[8,32,64,256]{3,2,1,0:T(8,128)} %bitcast.117, f32[8,32]{1,0:T(8,128)S(1)} %get-tuple-element.64), kind=kLoop, calls=%fused_computation | loop fusion | flops 7864320 | bytes 18875392 | tf_op jit(solution)/shard_map/reduce_sum | solution.py:70
  315.4 7.6 %all-gather.10.cloned.1.call-done = bf16[8224,256]{1,0:T(8,128)(2,1)} async-done(((bf16[2056,256]{1,0:T(8,128)(2,1)}), bf16[8224,256]{1,0:T(8,128)(2,1)}) %all-gather.10.cloned.1.call-update) | async-done | bytes 4210704 | tf_op jit(solution)/shard_map/all_gather | solution.py:167
  323.0 0.7 slice_convert_fusion.5
  324.1 3.2 multiply_reduce_fusion.2
  327.6 1.9 copy-done.1
  329.9 1.8 copy-done.2
  331.7 1.3 copy-done.4
  333.0 3.0 fusion.19
  336.0 3.3 copy.152
  339.8 1.1 copy-done.3
  340.9 1.4 multiply_reduce_fusion.3
  342.4 15.8 %convolution_convert_fusion = bf16[512,4096]{1,0:T(8,128)(2,1)} fusion(bf16[2048,4096]{1,0:T(8,128)(2,1)} %all-gather.6.cloned.1.call-done, f32[2048]{0:T(1024)S(1)} %copy-done.9, f32[512]{0:T(512)S(1)} %add_rsqrt_fusion, f32[512,2048]{0,1:T(8,128)S(1)} %bitcast.124, bf16[512,2048]{0,1:T(8,128)(2,1)S(1)} %copy-done.3), kind=kOutput, calls=%fused_computation.15 | convolution fusion | flops 8601468928 | bytes 27273216 | tf_op jit(solution)/shard_map/dot_general | solution.py:208
  358.2 41.6 %reduce-scatter.2.cloned.1.call-done = bf16[512,512]{1,0:T(8,128)(2,1)} async-done(((bf16[512,4096]{1,0:T(8,128)(2,1)}), bf16[512,512]{1,0:T(8,128)(2,1)}) %reduce-scatter.2.cloned.1.call-update) | async-done | bytes 524304 | tf_op jit(solution)/shard_map/reduce_scatter | solution.py:209
  (98 shorter events, 8.0 us)
Async XLA Ops:
  6.5 21.2 %copy-start.10 = (bf16[2048]{0:T(1024)(128)(2,1)S(1)}, bf16[2048]{0:T(1024)(128)(2,1)}, u32[]{:S(2)}) copy-start(bf16[2048]{0:T(1024)(128)(2,1)} %param.22) | copy-start | bytes 12292
  6.5 21.3 %copy-start.15 = (bf16[512]{0:T(512)(128)(2,1)S(1)}, bf16[512]{0:T(512)(128)(2,1)}, u32[]{:S(2)}) copy-start(bf16[512]{0:T(512)(128)(2,1)} %param.24) | copy-start | bytes 3076
  6.5 154.9 %all-gather.6.cloned.1.call-start = ((), (), s32[]{:S(2)}) async-start(), calls=%async_computation.1 | async-start | bytes 17301504 | tf_op jit(solution)/shard_map/all_gather | solution.py:102
  7.3 248.5 %all-gather.8.cloned.1.call-start = ((), (), s32[]{:S(2)}) async-start(), calls=%async_computation.3 | async-start | bytes 9474048 | tf_op jit(solution)/shard_map/all_gather | solution.py:158
  8.8 19.0 %collective-permute-start = (bf16[3,2560]{1,0:T(4,128)(2,1)S(1)}, bf16[3,2560]{1,0:T(4,128)(2,1)S(1)}, u32[]{:S(2)}, u32[]{:S(2)}) collective-permute-start(bf16[3,2560]{1,0:T(4,128)(2,1)S(1)} %pad_maximum_fusion.2), channel_id=1, source_target_pairs={{0,8},{8,16},{16,24},{24,32},{32,40},{40,48},{48,56},{56,64},{64,7... | collective-permute-start | bytes 46088 | tf_op jit(solution)/shard_map/ppermute | solution.py:111
  34.9 6.0 %copy-start.6 = (bf16[512,512]{1,0:T(8,128)(2,1)S(1)}, bf16[512,512]{1,0:T(8,128)(2,1)}, u32[]{:S(2)}) copy-start(bf16[512,512]{1,0:T(8,128)(2,1)} %param.19) | copy-start | bytes 1572868
  40.9 1.8 copy-start.7
  51.8 4.0 copy-start.14
  53.8 1.9 copy-start
  161.5 161.5 %all-gather.10.cloned.1.call-start = ((), (), s32[]{:S(2)}) async-start(), calls=%async_computation.4 | async-start | bytes 5263360 | tf_op jit(solution)/shard_map/all_gather | solution.py:167
  267.4 6.7 %copy-start.11 = (bf16[2048]{0:T(1024)(128)(2,1)S(1)}, bf16[2048]{0:T(1024)(128)(2,1)}, u32[]{:S(2)}) copy-start(bf16[2048]{0:T(1024)(128)(2,1)} %param.29) | copy-start | bytes 12292
  272.9 4.5 %copy-start.5 = (bf16[512,2048]{1,0:T(8,128)(2,1)S(1)}, bf16[512,2048]{1,0:T(8,128)(2,1)}, u32[]{:S(2)}) copy-start(bf16[512,2048]{1,0:T(8,128)(2,1)} %param.20) | copy-start | bytes 6291460
  274.0 125.8 %reduce-scatter.2.cloned.1.call-start = ((), (), s32[]{:S(2)}) async-start(), calls=%async_computation.2 | async-start | bytes 4718592 | tf_op jit(solution)/shard_map/reduce_scatter | solution.py:209
  277.4 2.5 copy-start.8
  327.3 2.2 copy-start.1
  327.3 2.2 copy-start.13
  329.5 2.2 copy-start.2
  329.5 3.5 copy-start.4
  329.5 3.5 copy-start.12
  339.3 1.6 copy-start.3
  339.8 2.6 copy-start.9
Sparse Core Ops, SparseCore 0:
  9.8 151.6 all-gather.5
  163.3 92.4 all-gather.7
  274.2 48.8 all-gather.9
  358.3 41.4 reduce-scatter.1

commit v7 on v3

--- a/solution.py
+++ b/solution.py
@@ -159,7 +159,10 @@
         shard_state = kept[c][..., None, None] * shard_state + chunk_states[c]
         shard_factor = shard_factor * kept[c]
 
-    row = gather_rows(pack_state(shard_state, shard_factor.reshape(-1)), "sz")
+    packed, weights = lax.optimization_barrier(
+        (pack_state(shard_state, shard_factor.reshape(-1)), weights)
+    )
+    row = gather_rows(packed, "sz")
     row_states, row_factors = unpack_state(row, heads)
     zpos = lax.axis_index("sz")
     in_row = combine(row_states, row_factors, zpos)

time: 478 us -> 503 us (1.052)
  waiting for transfers between devices: 309 us -> 338 us
    all_gather x1, waiting for transfers between devices: 0.02 us -> 105 us  [per_device(): weights = lax.all_gather(out_weight, SEQ, axis=1, tiled=True)]
    all_to_all x2, waiting for transfers between devices: 260 us -> 196 us  [gather_rows(): lax.all_to_all(jnp.broadcast_to(packed[None], (count,) + packed.shape), a...]
    reduce_scatter x1, waiting for transfers between devices: 48 us -> 35.9 us  [per_device(): lax.psum_scatter(partial_out.astype(jnp.bfloat16), 'head', scatter_dimens...]
  transfers between devices with their start and end apart: 5 -> 5, of which waited for: 3 -> 4; matrix products, arithmetic and copies ran while one was open for 23% -> 16% of each run, Pallas kernels for 0% -> 0%
where the time goes in v7:
time: 503 us; the launch traced here: 501 us
  waiting for transfers between devices  338 us (67%)
  local copies, waits for them, and re-layouts  46.2 us (9%)
  other arithmetic  45.8 us (9%)
  matrix products  42.6 us (8%)
  starting transfers between devices  14.9 us (3%)
  between operations  13.9 us (3%)
    all_to_all x2, waiting for transfers between devices, gather_rows(): lax.all_to_all(jnp.broadcast_to(packed[None], (count,) + packed.shape), a...  196 us
    all_gather x1, waiting for transfers between devices, per_device(): weights = lax.all_gather(out_weight, SEQ, axis=1, tiled=True)  105 us
    reduce_scatter x1, waiting for transfers between devices, per_device(): lax.psum_scatter(partial_out.astype(jnp.bfloat16), 'head', scatter_dimens...  35.9 us
    dot_general x1, matrix products, per_device(): jnp.einsum('ghcij,cjghp->cighp', decays * scores[:, None], scaled, precis...  21.5 us
    dot_general x1, matrix products, per_device(): partial_out = jnp.dot(normed, weights, preferred_element_type=jnp.float32)  15.8 us
    unnamed x29, local copies, waits for them, and re-layouts  15.4 us
    reduce_sum x2, other arithmetic, combine(): return jnp.sum(weights[:, :, None, None] * states, axis=0)  14.4 us
    convert_element_type x2, local copies, waits for them, and re-layouts, per_device(): u32 = u.astype(jnp.float32)  11.8 us
  transfers between devices with their start and end apart: 5, of which 4 were waited for; matrix products, arithmetic and copies ran while one was open for 16% of the time, Pallas kernels for 0%

profile of v7, /device:TPU:2, one launch (start us, length us, event | category | flops | bytes accessed | tf_op | source)
XLA Modules:
  0.0 501.5 jit_solution(15607240715031975150)
XLA Ops:
  6.5 0.7 all-gather.2.cloned.1.call-update
  7.3 0.7 slice.163
  8.0 0.8 slice.162
  8.8 3.8 collective-permute-start
  12.6 0.8 reduce-window.19
  14.8 1.0 compare_select_fusion
  16.6 1.2 reduce-window.20
  18.5 1.3 pad_add_fusion
  21.3 0.8 slice_convert_fusion.8
  22.5 0.9 slice_convert_fusion.3
  24.0 2.9 copy.117
  26.9 0.7 reshape.706
  28.1 6.8 %fusion.32 = f32[512,2048]{0,1:T(8,128)} fusion(bf16[512,2048]{0,1:T(8,128)(2,1)S(1)} %copy.117, f32[2048]{0:T(1024)S(1)} %bitcast.121, f32[512]{0:T(512)S(1)} %get-tuple-element.54, bf16[3,2048]{0,1:T(8,128)(2,1)S(1)} %copy.116, f32[2048]{0:T(1024)S(1)} %bitcast.122, f32[512]{0:T(512)S(1)} %get-tuple-element.55, f32[2048]{0:T(1024)S(1)} %bitcast.120, ...), kind=kLoop, calls=%fused_computation.55 | loop fusion | flops 31457280 | bytes 6350848 | tf_op jit(solution)/shard_map/convert_element_type | solution.py:146
  34.9 5.9 %reshape.725 = f32[2,256,32,64]{1,0,3,2:T(2,128)} reshape(f32[512,2048]{0,1:T(8,128)} %fusion.32) | data formatting | bytes 8388608 | tf_op jit(solution)/shard_map/convert_element_type | solution.py:146
  40.8 0.9 multiply_convert_fusion.3
  41.8 0.7 fusion.57
  42.5 9.0 %broadcast_multiply_fusion = (f32[2,256,32,64]{1,0,3,2:T(2,128)S(1)}, f32[2,256,32,64]{1,0,3,2:T(2,128)}) fusion(f32[2,256,32]{1,0,2:T(2,128)S(1)} %copy.130, f32[2,256,32,64]{1,0,3,2:T(2,128)} %reshape.725, f32[2,256,32]{1,0,2:T(2,128)S(1)} %bitcast.117), kind=kLoop, calls=%fused_computation.53 | loop fusion | flops 2097152 | bytes 12713984 | tf_op jit(solution)/shard_map/mul | solution.py:150
  51.6 2.1 fusion.22
  53.6 2.0 copy-done
  56.0 105.3 %all-gather.2.cloned.1.call-done = bf16[2048,4096]{1,0:T(8,128)(2,1)} async-done(((bf16[2048,128]{1,0:T(8,128)(2,1)}), bf16[2048,4096]{1,0:T(8,128)(2,1)}) %all-gather.2.cloned.1.call-update) | async-done | bytes 16777232 | tf_op jit(solution)/shard_map/all_gather | solution.py:109
  161.3 3.8 broadcast_in_dim.100
  165.0 5.1 %all-to-all-start = ((bf16[8,2056,256]{2,1,0:T(8,128)(2,1)}), bf16[8,2056,256]{2,1,0:T(8,128)(2,1)}, u32[]{:S(2)}, u32[]{:S(2)}) async-start(bf16[8,2056,256]{2,1,0:T(8,128)(2,1)} %broadcast_in_dim.100), calls=%async_computation | async-start | bytes 16842752 | tf_op jit(solution)/shard_map/all_to_all | solution.py:70
  170.3 184.3 %all-to-all-done = bf16[8,2056,256]{2,1,0:T(8,128)(2,1)} async-done(((bf16[8,2056,256]{2,1,0:T(8,128)(2,1)}), bf16[8,2056,256]{2,1,0:T(8,128)(2,1)}, u32[]{:S(2)}, u32[]{:S(2)}) %all-to-all-start) | async-done | bytes 8421408 | tf_op jit(solution)/shard_map/all_to_all | solution.py:70
  354.5 0.7 slice_reduce_fusion.2
  355.4 0.7 select_reduce_fusion.3
  356.4 0.7 mul.529
  357.1 11.2 %fusion = (bf16[2048,256]{1,0:T(8,128)(2,1)S(1)}, f32[2048,256]{1,0:T(8,128)S(1)}) fusion(f32[8,2048]{1,0:T(8,128)S(1)} %mul.520, bf16[8,2056,256]{2,1,0:T(8,128)(2,1)} %all-to-all-done, f32[8,2048]{1,0:T(8,128)} %mul.529), kind=kLoop, calls=%fused_computation.2 | loop fusion | flops 19922944 | bytes 11665408 | tf_op jit(solution)/shard_map/reduce_sum | solution.py:77
  368.3 2.2 broadcast_in_dim.171
  370.6 5.9 %all-to-all-start.1 = ((bf16[4,2056,256]{2,1,0:T(8,128)(2,1)}), bf16[4,2056,256]{2,1,0:T(8,128)(2,1)}, u32[]{:S(2)}, u32[]{:S(2)}) async-start(bf16[4,2056,256]{2,1,0:T(8,128)(2,1)} %broadcast_in_dim.171), calls=%async_computation.1 | async-start | bytes 8421376 | tf_op jit(solution)/shard_map/all_to_all | solution.py:70
  376.6 0.7 convert_element_type.184
  377.3 0.7 reshape.708
  377.9 0.8 broadcast.373
  378.7 1.0 copy.140
  379.9 4.0 copy.137
  384.1 5.9 %reshape.731 = f32[2,256,1,32,64]{1,0,4,3,2:T(2,128)} reshape(f32[512,2048]{0,1:T(8,128)} %fusion.32) | data formatting | bytes 8388608 | tf_op jit(solution)/shard_map/convert_element_type | solution.py:146
  390.2 21.5 %fusion.2 = f32[2,32,64,256]{3,2,1,0:T(8,128)} fusion(f32[2,256,256]{2,1,0:T(8,128)S(1)} %fusion.39, f32[32,2,256]{2,0,1:T(8,128)S(1)} %reduce_window_sum.47, pred[2,256,256]{2,1,0:T(8,128)(4,1)S(1)} %compare_and_fusion, f32[2,256,32,64]{1,0,3,2:T(2,128)} %get-tuple-element.40), kind=kOutput, calls=%fused_computation.4 | convolution fusion | flops 3238002688 | bytes 9109504 | tf_op jit(solution)/shard_map/ghcij,cjghp->cighp/dot_general | solution.py:188
  411.7 11.9 %all-to-all-done.1 = bf16[4,2056,256]{2,1,0:T(8,128)(2,1)} async-done(((bf16[4,2056,256]{2,1,0:T(8,128)(2,1)}), bf16[4,2056,256]{2,1,0:T(8,128)(2,1)}, u32[]{:S(2)}, u32[]{:S(2)}) %all-to-all-start.1) | async-done | bytes 4210720 | tf_op jit(solution)/shard_map/all_to_all | solution.py:70
  423.6 0.7 slice_convert_fusion.4
  424.7 3.2 multiply_reduce_fusion
  428.2 1.9 copy-done.1
  430.5 1.8 copy-done.2
  432.2 1.3 copy-done.4
  433.5 3.0 fusion.21
  436.6 3.3 copy.136
  440.4 1.1 copy-done.3
  441.5 1.4 multiply_reduce_fusion.1
  442.9 15.8 %convolution_convert_fusion = bf16[512,4096]{1,0:T(8,128)(2,1)} fusion(bf16[2048,4096]{1,0:T(8,128)(2,1)} %all-gather.2.cloned.1.call-done, f32[2048]{0:T(1024)S(1)} %convert_element_type.184, f32[512]{0:T(512)S(1)} %add_rsqrt_fusion, f32[512,2048]{0,1:T(8,128)S(1)} %bitcast.113, bf16[512,2048]{0,1:T(8,128)(2,1)S(1)} %copy-done.3), kind=kOutput, calls=%fused_computation.16 | convolution fusion | flops 8601468928 | bytes 27273216 | tf_op jit(solution)/shard_map/dot_general | solution.py:211
  458.7 35.9 %reduce-scatter.2.cloned.1.call-done = bf16[512,512]{1,0:T(8,128)(2,1)} async-done(((bf16[512,4096]{1,0:T(8,128)(2,1)}), bf16[512,512]{1,0:T(8,128)(2,1)}) %reduce-scatter.2.cloned.1.call-update) | async-done | bytes 524304 | tf_op jit(solution)/shard_map/reduce_scatter | solution.py:212
  (90 shorter events, 8.9 us)
Async XLA Ops:
  6.5 21.2 %copy-start.9 = (bf16[2048]{0:T(1024)(128)(2,1)S(1)}, bf16[2048]{0:T(1024)(128)(2,1)}, u32[]{:S(2)}) copy-start(bf16[2048]{0:T(1024)(128)(2,1)} %param.22) | copy-start | bytes 12292
  6.5 21.2 %copy-start.12 = (bf16[512]{0:T(512)(128)(2,1)S(1)}, bf16[512]{0:T(512)(128)(2,1)}, u32[]{:S(2)}) copy-start(bf16[512]{0:T(512)(128)(2,1)} %param.24) | copy-start | bytes 3076
  6.5 154.7 %all-gather.2.cloned.1.call-start = ((), (), s32[]{:S(2)}) async-start(), calls=%async_computation.3 | async-start | bytes 17301504 | tf_op jit(solution)/shard_map/all_gather | solution.py:109
  8.8 19.0 %collective-permute-start = (bf16[3,2560]{1,0:T(4,128)(2,1)S(1)}, bf16[3,2560]{1,0:T(4,128)(2,1)S(1)}, u32[]{:S(2)}, u32[]{:S(2)}) collective-permute-start(bf16[3,2560]{1,0:T(4,128)(2,1)S(1)} %pad_maximum_fusion.2), channel_id=1, source_target_pairs={{0,8},{8,16},{16,24},{24,32},{32,40},{40,48},{48,56},{56,64},{64,7... | collective-permute-start | bytes 46088 | tf_op jit(solution)/shard_map/ppermute | solution.py:118
  34.9 5.9 %copy-start.5 = (bf16[512,512]{1,0:T(8,128)(2,1)S(1)}, bf16[512,512]{1,0:T(8,128)(2,1)}, u32[]{:S(2)}) copy-start(bf16[512,512]{1,0:T(8,128)(2,1)} %param.19) | copy-start | bytes 1572868
  40.8 1.8 copy-start.6
  53.6 2.0 copy-start
  165.0 189.5 %all-to-all-start = ((bf16[8,2056,256]{2,1,0:T(8,128)(2,1)}), bf16[8,2056,256]{2,1,0:T(8,128)(2,1)}, u32[]{:S(2)}, u32[]{:S(2)}) async-start(bf16[8,2056,256]{2,1,0:T(8,128)(2,1)} %broadcast_in_dim.100), calls=%async_computation | async-start | bytes 16842752 | tf_op jit(solution)/shard_map/all_to_all | solution.py:70
  370.6 53.0 %all-to-all-start.1 = ((bf16[4,2056,256]{2,1,0:T(8,128)(2,1)}), bf16[4,2056,256]{2,1,0:T(8,128)(2,1)}, u32[]{:S(2)}, u32[]{:S(2)}) async-start(bf16[4,2056,256]{2,1,0:T(8,128)(2,1)} %broadcast_in_dim.171), calls=%async_computation.1 | async-start | bytes 8421376 | tf_op jit(solution)/shard_map/all_to_all | solution.py:70
  376.5 118.1 %reduce-scatter.2.cloned.1.call-start = ((), (), s32[]{:S(2)}) async-start(), calls=%async_computation.4 | async-start | bytes 4718592 | tf_op jit(solution)/shard_map/reduce_scatter | solution.py:212
  379.9 4.0 copy-start.7
  411.7 16.2 %copy-start.8 = (f32[32]{0:T(128)S(1)}, f32[32]{0:T(128)}, u32[]{:S(2)}) copy-start(f32[32]{0:T(128)} %get-tuple-element.61) | copy-start | bytes 388
  427.9 2.2 copy-start.1
  427.9 2.2 copy-start.11
  430.1 2.2 copy-start.2
  430.1 3.5 copy-start.4
  430.1 3.5 copy-start.10
  439.9 1.6 copy-start.3
Sparse Core Ops, SparseCore 0:
  9.8 151.4 all-gather.1
  458.8 35.7 reduce-scatter.1
